TPU v7x, 64 devices: a 2x2x8 block of a 4x4x8 slice. The times are simulated.
64 devices in a mesh: dp: 4 (over x, y), cp: 16 (over z, core).
Axes of the slice: x: 2, y: 2, z: 8, core: 2. Of those that a mesh axis runs over, the one named last changes fastest.
The devices are a block of a 4x4x8 slice.
Arguments:
- queries: bfloat16 [8, 6144, 4, 256], P('dp', 'cp'), parts along dimension 0
- keys: bfloat16 [8, 6144, 1, 256], P('dp', 'cp'), parts along dimension 0
- values: bfloat16 [8, 6144, 1, 256], P('dp', 'cp'), parts along dimension 0
- out_grad: bfloat16 [8, 6144, 4, 256], P('dp', 'cp'), parts along dimension 0
Outputs:
- output 1: bfloat16 [8, 6144, 4, 256], P('dp', 'cp'), parts along dimension 0
- output 2: float32 [8, 4, 6144], P('dp', None, 'cp'), parts along dimension 0
- output 3: bfloat16 [8, 6144, 4, 256], P('dp', 'cp'), parts along dimension 0
- output 4: bfloat16 [8, 6144, 1, 256], P('dp', 'cp'), parts along dimension 0
- output 5: bfloat16 [8, 6144, 1, 256], P('dp', 'cp'), parts along dimension 0
There are 4 independent parts. A program takes and returns all parts, laid end to end along the dimension named above; each array names one.
All inputs are finite; a program needn't handle non-finite values.
Results may differ from a plain program's by a relative error of at most 0.0185315.
Values are sent between devices in bfloat16 or wider.
A program may use at most 768 MiB of HBM per device.

v0:
```python
import jax
import jax.numpy as jnp
from jax import lax
from jax.sharding import PartitionSpec as P


def block_scores(query5, key_blk, scale, causal):
    scores = jnp.einsum("bqgrd,bkgd->bgrqk", query5, key_blk, preferred_element_type=jnp.float32) * scale
    if causal:
        tokens = query5.shape[1]
        row_idx = lax.broadcasted_iota(jnp.int32, (tokens, tokens), 0)
        col_idx = lax.broadcasted_iota(jnp.int32, (tokens, tokens), 1)
        scores = jnp.where(row_idx >= col_idx, scores, -jnp.inf)
    return scores


def forward_step(query5, key_blk, value_blk, state, scale, causal):
    run_max, run_sum, run_acc = state
    scores = block_scores(query5, key_blk, scale, causal)
    new_max = jnp.maximum(run_max, jnp.max(scores, axis=-1))
    alpha = jnp.exp(run_max - new_max)
    weights = jnp.exp(scores - new_max[..., None])
    new_sum = run_sum * alpha + jnp.sum(weights, axis=-1)
    new_acc = run_acc * alpha[..., None] + jnp.einsum("bgrqk,bkgd->bgrqd", weights.astype(jnp.bfloat16), value_blk, preferred_element_type=jnp.float32)
    return new_max, new_sum, new_acc


def backward_step(query5, grad5, row_lse, delta, key_blk, value_blk, scale, causal):
    scores = block_scores(query5, key_blk, scale, causal)
    prob_mat = jnp.exp(scores - row_lse[..., None])
    grad_prob = jnp.einsum("bqgrd,bkgd->bgrqk", grad5, value_blk, preferred_element_type=jnp.float32)
    grad_score = (prob_mat * (grad_prob - delta[..., None])).astype(jnp.bfloat16)
    prob_low = prob_mat.astype(jnp.bfloat16)
    dq_part = jnp.einsum("bgrqk,bkgd->bqgrd", grad_score, key_blk, preferred_element_type=jnp.float32) * scale
    dk_part = jnp.einsum("bgrqk,bqgrd->bkgd", grad_score, query5, preferred_element_type=jnp.float32) * scale
    dv_part = jnp.einsum("bgrqk,bqgrd->bkgd", prob_low, grad5, preferred_element_type=jnp.float32)
    return dq_part, dk_part, dv_part


def solution(mesh):
    cp_size = mesh.shape["cp"]
    shift_pairs = [(source, (source + 1) % cp_size) for source in range(cp_size)]

    def attention_shard(queries, keys, values, out_grad):
        batch, tokens, heads, head_dim = queries.shape
        kv_heads = keys.shape[2]
        ratio = heads // kv_heads
        scale = head_dim ** -0.5
        cp_rank = lax.axis_index("cp")
        query5 = queries.reshape(batch, tokens, kv_heads, ratio, head_dim)
        grad5 = out_grad.reshape(batch, tokens, kv_heads, ratio, head_dim)
        stat_shape = (batch, kv_heads, ratio, tokens)
        init_state = (jnp.full(stat_shape, -jnp.inf, jnp.float32), jnp.zeros(stat_shape, jnp.float32), jnp.zeros(stat_shape + (head_dim,), jnp.float32))
        diag_state = forward_step(query5, keys, values, init_state, scale, True)

        def forward_body(step, carry):
            key_cur, value_cur, state = carry
            key_cur = lax.ppermute(key_cur, "cp", shift_pairs)
            value_cur = lax.ppermute(value_cur, "cp", shift_pairs)
            state = lax.cond(step <= cp_rank, lambda prev: forward_step(query5, key_cur, value_cur, prev, scale, False), lambda prev: prev, state)
            return key_cur, value_cur, state

        run_max, run_sum, run_acc = lax.fori_loop(1, cp_size, forward_body, (keys, values, diag_state))[2]
        out5 = (run_acc / run_sum[..., None]).astype(jnp.bfloat16)
        attn_out = jnp.transpose(out5, (0, 3, 1, 2, 4)).reshape(batch, tokens, heads, head_dim)
        row_lse = run_max + jnp.log(run_sum)
        delta = jnp.einsum("bqgrd,bgrqd->bgrq", grad5, out5, preferred_element_type=jnp.float32)

        dq_diag, dk_diag, dv_diag = backward_step(query5, grad5, row_lse, delta, keys, values, scale, True)

        def backward_body(step, carry):
            key_cur, value_cur, dk_cur, dv_cur, dq_acc = carry
            key_cur = lax.ppermute(key_cur, "cp", shift_pairs)
            value_cur = lax.ppermute(value_cur, "cp", shift_pairs)
            dk_cur = lax.ppermute(dk_cur, "cp", shift_pairs)
            dv_cur = lax.ppermute(dv_cur, "cp", shift_pairs)

            def visit(acc_in):
                dk_in, dv_in, dq_in = acc_in
                dq_part, dk_part, dv_part = backward_step(query5, grad5, row_lse, delta, key_cur, value_cur, scale, False)
                return dk_in + dk_part, dv_in + dv_part, dq_in + dq_part

            dk_cur, dv_cur, dq_acc = lax.cond(step <= cp_rank, visit, lambda acc_in: acc_in, (dk_cur, dv_cur, dq_acc))
            return key_cur, value_cur, dk_cur, dv_cur, dq_acc

        carry_out = lax.fori_loop(1, cp_size, backward_body, (keys, values, dk_diag, dv_diag, dq_diag))
        dk_home = lax.ppermute(carry_out[2], "cp", shift_pairs)
        dv_home = lax.ppermute(carry_out[3], "cp", shift_pairs)
        grad_query = carry_out[4].reshape(batch, tokens, heads, head_dim).astype(jnp.bfloat16)
        return attn_out, row_lse.reshape(batch, heads, tokens), grad_query, dk_home.astype(jnp.bfloat16), dv_home.astype(jnp.bfloat16)

    seq_spec = P("dp", "cp")
    return jax.shard_map(attention_shard, mesh=mesh, in_specs=(seq_spec, seq_spec, seq_spec, seq_spec), out_specs=(seq_spec, P("dp", None, "cp"), seq_spec, seq_spec, seq_spec), check_vma=False)
```

profile of v0, /device:TPU:254, one launch (start us, length us, event | category | flops | bytes accessed | tf_op | source)
XLA Modules:
  0.0 1035.0 jit_solution(6713064690880008880)
XLA Ops:
  12.8 310.0 %while.42 = (s32[]{:T(128)}, bf16[2,384,1,256]{3,1,0,2:T(8,128)(2,1)}, bf16[2,384,1,256]{3,1,0,2:T(8,128)(2,1)}, f32[2,1,4,384]{3,2,0,1:T(4,128)S(1)}, f32[2,1,4...) while((s32[]{:T(128)}, ...), condition=%wide.region_7.8_spmd, body=%wide.region_2.7_spmd.sunk | while | flops 1218978816 | bytes 52986256 | solution.py:63
  346.7 674.2 %while.43 = (s32[]{:T(128)}, bf16[2,384,1,256]{3,1,0,2:T(8,128)(2,1)}, bf16[2,384,1,256]{3,1,0,2:T(8,128)(2,1)}, f32[2,384,1,256]{3,1,0,2:T(8,128)}, f32[2,384,1...) while((s32[]{:T(128)}, ...), condition=%wide.region_11.12_spmd, body=%wide.region_8.11_spmd.sunk | while | flops 3031498752 | bytes 77697616 | solution.py:86
  347.3 23.5 %collective-permute-done.2 = bf16[2,384,1,256]{3,1,0,2:T(8,128)(2,1)S(1)} collective-permute-done((bf16[2,384,1,256]{3,1,0,2:T(8,128)(2,1)}, bf16[2,384,1,256]{3,1,0,2:T(8,128)(2,1)S(1)}, u32[]{:S(2)}, u32[]{:S(2)}) %collective-permute-start.2) | collective-permute-done | bytes 393248 | tf_op jit(solution)/shard_map/while/body/eval_jaxpr/ppermute | solution.py:73
  393.0 23.5 %collective-permute-done.2 = bf16[2,384,1,256]{3,1,0,2:T(8,128)(2,1)S(1)} collective-permute-done((bf16[2,384,1,256]{3,1,0,2:T(8,128)(2,1)}, bf16[2,384,1,256]{3,1,0,2:T(8,128)(2,1)S(1)}, u32[]{:S(2)}, u32[]{:S(2)}) %collective-permute-start.2) | collective-permute-done | bytes 393248 | tf_op jit(solution)/shard_map/while/body/eval_jaxpr/ppermute | solution.py:73
  422.5 11.4 %conditional.5 = ((f32[2,384,1,256]{3,1,0,2:T(8,128)}, f32[2,384,1,256]{3,1,0,2:T(8,128)}, f32[2,384,1,4,256]{4,1,3,0,2:T(8,128)})) conditional(s32[]{:T(128)} %convert_element_type.93, (f32[2,384,1,256]{3,1,0,2:T(8,128)}, f32[2,384,1,256]{3,1,0,2:T(8,128)}, f32[2,384,1,4,256]{4,1,3,0,2:T(8,128)}) %tuple.82, ...), branch_computations={%region_9.9_spmd, %region_10.10_spmd} | conditional | flops 3031498752 | bytes 63443088 | solution.py:83
  438.7 23.5 %collective-permute-done.2 = bf16[2,384,1,256]{3,1,0,2:T(8,128)(2,1)S(1)} collective-permute-done((bf16[2,384,1,256]{3,1,0,2:T(8,128)(2,1)}, bf16[2,384,1,256]{3,1,0,2:T(8,128)(2,1)S(1)}, u32[]{:S(2)}, u32[]{:S(2)}) %collective-permute-start.2) | collective-permute-done | bytes 393248 | tf_op jit(solution)/shard_map/while/body/eval_jaxpr/ppermute | solution.py:73
  484.4 23.5 %collective-permute-done.2 = bf16[2,384,1,256]{3,1,0,2:T(8,128)(2,1)S(1)} collective-permute-done((bf16[2,384,1,256]{3,1,0,2:T(8,128)(2,1)}, bf16[2,384,1,256]{3,1,0,2:T(8,128)(2,1)S(1)}, u32[]{:S(2)}, u32[]{:S(2)}) %collective-permute-start.2) | collective-permute-done | bytes 393248 | tf_op jit(solution)/shard_map/while/body/eval_jaxpr/ppermute | solution.py:73
  513.9 11.4 %conditional.5 = ((f32[2,384,1,256]{3,1,0,2:T(8,128)}, f32[2,384,1,256]{3,1,0,2:T(8,128)}, f32[2,384,1,4,256]{4,1,3,0,2:T(8,128)})) conditional(s32[]{:T(128)} %convert_element_type.93, (f32[2,384,1,256]{3,1,0,2:T(8,128)}, f32[2,384,1,256]{3,1,0,2:T(8,128)}, f32[2,384,1,4,256]{4,1,3,0,2:T(8,128)}) %tuple.82, ...), branch_computations={%region_9.9_spmd, %region_10.10_spmd} | conditional | flops 3031498752 | bytes 63443088 | solution.py:83
  530.2 23.5 %collective-permute-done.2 = bf16[2,384,1,256]{3,1,0,2:T(8,128)(2,1)S(1)} collective-permute-done((bf16[2,384,1,256]{3,1,0,2:T(8,128)(2,1)}, bf16[2,384,1,256]{3,1,0,2:T(8,128)(2,1)S(1)}, u32[]{:S(2)}, u32[]{:S(2)}) %collective-permute-start.2) | collective-permute-done | bytes 393248 | tf_op jit(solution)/shard_map/while/body/eval_jaxpr/ppermute | solution.py:73
  559.6 11.4 %conditional.5 = ((f32[2,384,1,256]{3,1,0,2:T(8,128)}, f32[2,384,1,256]{3,1,0,2:T(8,128)}, f32[2,384,1,4,256]{4,1,3,0,2:T(8,128)})) conditional(s32[]{:T(128)} %convert_element_type.93, (f32[2,384,1,256]{3,1,0,2:T(8,128)}, f32[2,384,1,256]{3,1,0,2:T(8,128)}, f32[2,384,1,4,256]{4,1,3,0,2:T(8,128)}) %tuple.82, ...), branch_computations={%region_9.9_spmd, %region_10.10_spmd} | conditional | flops 3031498752 | bytes 63443088 | solution.py:83
  575.9 23.5 %collective-permute-done.2 = bf16[2,384,1,256]{3,1,0,2:T(8,128)(2,1)S(1)} collective-permute-done((bf16[2,384,1,256]{3,1,0,2:T(8,128)(2,1)}, bf16[2,384,1,256]{3,1,0,2:T(8,128)(2,1)S(1)}, u32[]{:S(2)}, u32[]{:S(2)}) %collective-permute-start.2) | collective-permute-done | bytes 393248 | tf_op jit(solution)/shard_map/while/body/eval_jaxpr/ppermute | solution.py:73
  621.6 23.5 %collective-permute-done.2 = bf16[2,384,1,256]{3,1,0,2:T(8,128)(2,1)S(1)} collective-permute-done((bf16[2,384,1,256]{3,1,0,2:T(8,128)(2,1)}, bf16[2,384,1,256]{3,1,0,2:T(8,128)(2,1)S(1)}, u32[]{:S(2)}, u32[]{:S(2)}) %collective-permute-start.2) | collective-permute-done | bytes 393248 | tf_op jit(solution)/shard_map/while/body/eval_jaxpr/ppermute | solution.py:73
  651.0 11.4 %conditional.5 = ((f32[2,384,1,256]{3,1,0,2:T(8,128)}, f32[2,384,1,256]{3,1,0,2:T(8,128)}, f32[2,384,1,4,256]{4,1,3,0,2:T(8,128)})) conditional(s32[]{:T(128)} %convert_element_type.93, (f32[2,384,1,256]{3,1,0,2:T(8,128)}, f32[2,384,1,256]{3,1,0,2:T(8,128)}, f32[2,384,1,4,256]{4,1,3,0,2:T(8,128)}) %tuple.82, ...), branch_computations={%region_9.9_spmd, %region_10.10_spmd} | conditional | flops 3031498752 | bytes 63443088 | solution.py:83
  667.3 23.5 %collective-permute-done.2 = bf16[2,384,1,256]{3,1,0,2:T(8,128)(2,1)S(1)} collective-permute-done((bf16[2,384,1,256]{3,1,0,2:T(8,128)(2,1)}, bf16[2,384,1,256]{3,1,0,2:T(8,128)(2,1)S(1)}, u32[]{:S(2)}, u32[]{:S(2)}) %collective-permute-start.2) | collective-permute-done | bytes 393248 | tf_op jit(solution)/shard_map/while/body/eval_jaxpr/ppermute | solution.py:73
  696.8 11.4 %conditional.5 = ((f32[2,384,1,256]{3,1,0,2:T(8,128)}, f32[2,384,1,256]{3,1,0,2:T(8,128)}, f32[2,384,1,4,256]{4,1,3,0,2:T(8,128)})) conditional(s32[]{:T(128)} %convert_element_type.93, (f32[2,384,1,256]{3,1,0,2:T(8,128)}, f32[2,384,1,256]{3,1,0,2:T(8,128)}, f32[2,384,1,4,256]{4,1,3,0,2:T(8,128)}) %tuple.82, ...), branch_computations={%region_9.9_spmd, %region_10.10_spmd} | conditional | flops 3031498752 | bytes 63443088 | solution.py:83
  713.0 23.5 %collective-permute-done.2 = bf16[2,384,1,256]{3,1,0,2:T(8,128)(2,1)S(1)} collective-permute-done((bf16[2,384,1,256]{3,1,0,2:T(8,128)(2,1)}, bf16[2,384,1,256]{3,1,0,2:T(8,128)(2,1)S(1)}, u32[]{:S(2)}, u32[]{:S(2)}) %collective-permute-start.2) | collective-permute-done | bytes 393248 | tf_op jit(solution)/shard_map/while/body/eval_jaxpr/ppermute | solution.py:73
  758.7 23.5 %collective-permute-done.2 = bf16[2,384,1,256]{3,1,0,2:T(8,128)(2,1)S(1)} collective-permute-done((bf16[2,384,1,256]{3,1,0,2:T(8,128)(2,1)}, bf16[2,384,1,256]{3,1,0,2:T(8,128)(2,1)S(1)}, u32[]{:S(2)}, u32[]{:S(2)}) %collective-permute-start.2) | collective-permute-done | bytes 393248 | tf_op jit(solution)/shard_map/while/body/eval_jaxpr/ppermute | solution.py:73
  788.2 11.4 %conditional.5 = ((f32[2,384,1,256]{3,1,0,2:T(8,128)}, f32[2,384,1,256]{3,1,0,2:T(8,128)}, f32[2,384,1,4,256]{4,1,3,0,2:T(8,128)})) conditional(s32[]{:T(128)} %convert_element_type.93, (f32[2,384,1,256]{3,1,0,2:T(8,128)}, f32[2,384,1,256]{3,1,0,2:T(8,128)}, f32[2,384,1,4,256]{4,1,3,0,2:T(8,128)}) %tuple.82, ...), branch_computations={%region_9.9_spmd, %region_10.10_spmd} | conditional | flops 3031498752 | bytes 63443088 | solution.py:83
  804.4 23.5 %collective-permute-done.2 = bf16[2,384,1,256]{3,1,0,2:T(8,128)(2,1)S(1)} collective-permute-done((bf16[2,384,1,256]{3,1,0,2:T(8,128)(2,1)}, bf16[2,384,1,256]{3,1,0,2:T(8,128)(2,1)S(1)}, u32[]{:S(2)}, u32[]{:S(2)}) %collective-permute-start.2) | collective-permute-done | bytes 393248 | tf_op jit(solution)/shard_map/while/body/eval_jaxpr/ppermute | solution.py:73
  833.9 11.4 %conditional.5 = ((f32[2,384,1,256]{3,1,0,2:T(8,128)}, f32[2,384,1,256]{3,1,0,2:T(8,128)}, f32[2,384,1,4,256]{4,1,3,0,2:T(8,128)})) conditional(s32[]{:T(128)} %convert_element_type.93, (f32[2,384,1,256]{3,1,0,2:T(8,128)}, f32[2,384,1,256]{3,1,0,2:T(8,128)}, f32[2,384,1,4,256]{4,1,3,0,2:T(8,128)}) %tuple.82, ...), branch_computations={%region_9.9_spmd, %region_10.10_spmd} | conditional | flops 3031498752 | bytes 63443088 | solution.py:83
  850.1 23.5 %collective-permute-done.2 = bf16[2,384,1,256]{3,1,0,2:T(8,128)(2,1)S(1)} collective-permute-done((bf16[2,384,1,256]{3,1,0,2:T(8,128)(2,1)}, bf16[2,384,1,256]{3,1,0,2:T(8,128)(2,1)S(1)}, u32[]{:S(2)}, u32[]{:S(2)}) %collective-permute-start.2) | collective-permute-done | bytes 393248 | tf_op jit(solution)/shard_map/while/body/eval_jaxpr/ppermute | solution.py:73
  895.8 23.5 %collective-permute-done.2 = bf16[2,384,1,256]{3,1,0,2:T(8,128)(2,1)S(1)} collective-permute-done((bf16[2,384,1,256]{3,1,0,2:T(8,128)(2,1)}, bf16[2,384,1,256]{3,1,0,2:T(8,128)(2,1)S(1)}, u32[]{:S(2)}, u32[]{:S(2)}) %collective-permute-start.2) | collective-permute-done | bytes 393248 | tf_op jit(solution)/shard_map/while/body/eval_jaxpr/ppermute | solution.py:73
  941.5 23.5 %collective-permute-done.2 = bf16[2,384,1,256]{3,1,0,2:T(8,128)(2,1)S(1)} collective-permute-done((bf16[2,384,1,256]{3,1,0,2:T(8,128)(2,1)}, bf16[2,384,1,256]{3,1,0,2:T(8,128)(2,1)S(1)}, u32[]{:S(2)}, u32[]{:S(2)}) %collective-permute-start.2) | collective-permute-done | bytes 393248 | tf_op jit(solution)/shard_map/while/body/eval_jaxpr/ppermute | solution.py:73
  987.2 23.5 %collective-permute-done.2 = bf16[2,384,1,256]{3,1,0,2:T(8,128)(2,1)S(1)} collective-permute-done((bf16[2,384,1,256]{3,1,0,2:T(8,128)(2,1)}, bf16[2,384,1,256]{3,1,0,2:T(8,128)(2,1)S(1)}, u32[]{:S(2)}, u32[]{:S(2)}) %collective-permute-start.2) | collective-permute-done | bytes 393248 | tf_op jit(solution)/shard_map/while/body/eval_jaxpr/ppermute | solution.py:73
  (771 shorter events, 861.2 us)
Async XLA Ops:
  346.7 30.1 %collective-permute-start.4 = (f32[2,384,1,256]{3,1,0,2:T(8,128)}, f32[2,384,1,256]{3,1,0,2:T(8,128)}, u32[]{:S(2)}, u32[]{:S(2)}) collective-permute-start(f32[2,384,1,256]{3,1,0,2:T(8,128)} %get-tuple-element.662), channel_id=1, source_target_pairs={{0,1},{1,2},{2,3},{3,4},{4,5},{5,6},{6,7},{7,8},{8,9},{9,10},{10,1... | collective-permute-start | bytes 2359304 | tf_op jit(solution)/shard_map/while/body/eval_jaxpr/ppermute | solution.py:75
  346.7 30.1 %collective-permute-start.5 = (f32[2,384,1,256]{3,1,0,2:T(8,128)}, f32[2,384,1,256]{3,1,0,2:T(8,128)}, u32[]{:S(2)}, u32[]{:S(2)}) collective-permute-start(f32[2,384,1,256]{3,1,0,2:T(8,128)} %get-tuple-element.663), channel_id=1, source_target_pairs={{0,1},{1,2},{2,3},{3,4},{4,5},{5,6},{6,7},{7,8},{8,9},{9,10},{10,1... | collective-permute-start | bytes 2359304 | tf_op jit(solution)/shard_map/while/body/eval_jaxpr/ppermute | solution.py:76
  392.4 30.1 %collective-permute-start.4 = (f32[2,384,1,256]{3,1,0,2:T(8,128)}, f32[2,384,1,256]{3,1,0,2:T(8,128)}, u32[]{:S(2)}, u32[]{:S(2)}) collective-permute-start(f32[2,384,1,256]{3,1,0,2:T(8,128)} %get-tuple-element.662), channel_id=1, source_target_pairs={{0,1},{1,2},{2,3},{3,4},{4,5},{5,6},{6,7},{7,8},{8,9},{9,10},{10,1... | collective-permute-start | bytes 2359304 | tf_op jit(solution)/shard_map/while/body/eval_jaxpr/ppermute | solution.py:75
  392.4 30.1 %collective-permute-start.5 = (f32[2,384,1,256]{3,1,0,2:T(8,128)}, f32[2,384,1,256]{3,1,0,2:T(8,128)}, u32[]{:S(2)}, u32[]{:S(2)}) collective-permute-start(f32[2,384,1,256]{3,1,0,2:T(8,128)} %get-tuple-element.663), channel_id=1, source_target_pairs={{0,1},{1,2},{2,3},{3,4},{4,5},{5,6},{6,7},{7,8},{8,9},{9,10},{10,1... | collective-permute-start | bytes 2359304 | tf_op jit(solution)/shard_map/while/body/eval_jaxpr/ppermute | solution.py:76
  438.1 30.1 %collective-permute-start.4 = (f32[2,384,1,256]{3,1,0,2:T(8,128)}, f32[2,384,1,256]{3,1,0,2:T(8,128)}, u32[]{:S(2)}, u32[]{:S(2)}) collective-permute-start(f32[2,384,1,256]{3,1,0,2:T(8,128)} %get-tuple-element.662), channel_id=1, source_target_pairs={{0,1},{1,2},{2,3},{3,4},{4,5},{5,6},{6,7},{7,8},{8,9},{9,10},{10,1... | collective-permute-start | bytes 2359304 | tf_op jit(solution)/shard_map/while/body/eval_jaxpr/ppermute | solution.py:75
  483.8 30.1 %collective-permute-start.4 = (f32[2,384,1,256]{3,1,0,2:T(8,128)}, f32[2,384,1,256]{3,1,0,2:T(8,128)}, u32[]{:S(2)}, u32[]{:S(2)}) collective-permute-start(f32[2,384,1,256]{3,1,0,2:T(8,128)} %get-tuple-element.662), channel_id=1, source_target_pairs={{0,1},{1,2},{2,3},{3,4},{4,5},{5,6},{6,7},{7,8},{8,9},{9,10},{10,1... | collective-permute-start | bytes 2359304 | tf_op jit(solution)/shard_map/while/body/eval_jaxpr/ppermute | solution.py:75
  483.8 30.1 %collective-permute-start.5 = (f32[2,384,1,256]{3,1,0,2:T(8,128)}, f32[2,384,1,256]{3,1,0,2:T(8,128)}, u32[]{:S(2)}, u32[]{:S(2)}) collective-permute-start(f32[2,384,1,256]{3,1,0,2:T(8,128)} %get-tuple-element.663), channel_id=1, source_target_pairs={{0,1},{1,2},{2,3},{3,4},{4,5},{5,6},{6,7},{7,8},{8,9},{9,10},{10,1... | collective-permute-start | bytes 2359304 | tf_op jit(solution)/shard_map/while/body/eval_jaxpr/ppermute | solution.py:76
  529.5 30.1 %collective-permute-start.4 = (f32[2,384,1,256]{3,1,0,2:T(8,128)}, f32[2,384,1,256]{3,1,0,2:T(8,128)}, u32[]{:S(2)}, u32[]{:S(2)}) collective-permute-start(f32[2,384,1,256]{3,1,0,2:T(8,128)} %get-tuple-element.662), channel_id=1, source_target_pairs={{0,1},{1,2},{2,3},{3,4},{4,5},{5,6},{6,7},{7,8},{8,9},{9,10},{10,1... | collective-permute-start | bytes 2359304 | tf_op jit(solution)/shard_map/while/body/eval_jaxpr/ppermute | solution.py:75
  529.6 30.1 %collective-permute-start.5 = (f32[2,384,1,256]{3,1,0,2:T(8,128)}, f32[2,384,1,256]{3,1,0,2:T(8,128)}, u32[]{:S(2)}, u32[]{:S(2)}) collective-permute-start(f32[2,384,1,256]{3,1,0,2:T(8,128)} %get-tuple-element.663), channel_id=1, source_target_pairs={{0,1},{1,2},{2,3},{3,4},{4,5},{5,6},{6,7},{7,8},{8,9},{9,10},{10,1... | collective-permute-start | bytes 2359304 | tf_op jit(solution)/shard_map/while/body/eval_jaxpr/ppermute | solution.py:76
  575.3 30.1 %collective-permute-start.4 = (f32[2,384,1,256]{3,1,0,2:T(8,128)}, f32[2,384,1,256]{3,1,0,2:T(8,128)}, u32[]{:S(2)}, u32[]{:S(2)}) collective-permute-start(f32[2,384,1,256]{3,1,0,2:T(8,128)} %get-tuple-element.662), channel_id=1, source_target_pairs={{0,1},{1,2},{2,3},{3,4},{4,5},{5,6},{6,7},{7,8},{8,9},{9,10},{10,1... | collective-permute-start | bytes 2359304 | tf_op jit(solution)/shard_map/while/body/eval_jaxpr/ppermute | solution.py:75
  621.0 30.1 %collective-permute-start.4 = (f32[2,384,1,256]{3,1,0,2:T(8,128)}, f32[2,384,1,256]{3,1,0,2:T(8,128)}, u32[]{:S(2)}, u32[]{:S(2)}) collective-permute-start(f32[2,384,1,256]{3,1,0,2:T(8,128)} %get-tuple-element.662), channel_id=1, source_target_pairs={{0,1},{1,2},{2,3},{3,4},{4,5},{5,6},{6,7},{7,8},{8,9},{9,10},{10,1... | collective-permute-start | bytes 2359304 | tf_op jit(solution)/shard_map/while/body/eval_jaxpr/ppermute | solution.py:75
  621.0 30.1 %collective-permute-start.5 = (f32[2,384,1,256]{3,1,0,2:T(8,128)}, f32[2,384,1,256]{3,1,0,2:T(8,128)}, u32[]{:S(2)}, u32[]{:S(2)}) collective-permute-start(f32[2,384,1,256]{3,1,0,2:T(8,128)} %get-tuple-element.663), channel_id=1, source_target_pairs={{0,1},{1,2},{2,3},{3,4},{4,5},{5,6},{6,7},{7,8},{8,9},{9,10},{10,1... | collective-permute-start | bytes 2359304 | tf_op jit(solution)/shard_map/while/body/eval_jaxpr/ppermute | solution.py:76
  666.7 30.1 %collective-permute-start.4 = (f32[2,384,1,256]{3,1,0,2:T(8,128)}, f32[2,384,1,256]{3,1,0,2:T(8,128)}, u32[]{:S(2)}, u32[]{:S(2)}) collective-permute-start(f32[2,384,1,256]{3,1,0,2:T(8,128)} %get-tuple-element.662), channel_id=1, source_target_pairs={{0,1},{1,2},{2,3},{3,4},{4,5},{5,6},{6,7},{7,8},{8,9},{9,10},{10,1... | collective-permute-start | bytes 2359304 | tf_op jit(solution)/shard_map/while/body/eval_jaxpr/ppermute | solution.py:75
  666.7 30.1 %collective-permute-start.5 = (f32[2,384,1,256]{3,1,0,2:T(8,128)}, f32[2,384,1,256]{3,1,0,2:T(8,128)}, u32[]{:S(2)}, u32[]{:S(2)}) collective-permute-start(f32[2,384,1,256]{3,1,0,2:T(8,128)} %get-tuple-element.663), channel_id=1, source_target_pairs={{0,1},{1,2},{2,3},{3,4},{4,5},{5,6},{6,7},{7,8},{8,9},{9,10},{10,1... | collective-permute-start | bytes 2359304 | tf_op jit(solution)/shard_map/while/body/eval_jaxpr/ppermute | solution.py:76
  712.4 30.1 %collective-permute-start.4 = (f32[2,384,1,256]{3,1,0,2:T(8,128)}, f32[2,384,1,256]{3,1,0,2:T(8,128)}, u32[]{:S(2)}, u32[]{:S(2)}) collective-permute-start(f32[2,384,1,256]{3,1,0,2:T(8,128)} %get-tuple-element.662), channel_id=1, source_target_pairs={{0,1},{1,2},{2,3},{3,4},{4,5},{5,6},{6,7},{7,8},{8,9},{9,10},{10,1... | collective-permute-start | bytes 2359304 | tf_op jit(solution)/shard_map/while/body/eval_jaxpr/ppermute | solution.py:75
  758.1 30.1 %collective-permute-start.4 = (f32[2,384,1,256]{3,1,0,2:T(8,128)}, f32[2,384,1,256]{3,1,0,2:T(8,128)}, u32[]{:S(2)}, u32[]{:S(2)}) collective-permute-start(f32[2,384,1,256]{3,1,0,2:T(8,128)} %get-tuple-element.662), channel_id=1, source_target_pairs={{0,1},{1,2},{2,3},{3,4},{4,5},{5,6},{6,7},{7,8},{8,9},{9,10},{10,1... | collective-permute-start | bytes 2359304 | tf_op jit(solution)/shard_map/while/body/eval_jaxpr/ppermute | solution.py:75
  758.1 30.1 %collective-permute-start.5 = (f32[2,384,1,256]{3,1,0,2:T(8,128)}, f32[2,384,1,256]{3,1,0,2:T(8,128)}, u32[]{:S(2)}, u32[]{:S(2)}) collective-permute-start(f32[2,384,1,256]{3,1,0,2:T(8,128)} %get-tuple-element.663), channel_id=1, source_target_pairs={{0,1},{1,2},{2,3},{3,4},{4,5},{5,6},{6,7},{7,8},{8,9},{9,10},{10,1... | collective-permute-start | bytes 2359304 | tf_op jit(solution)/shard_map/while/body/eval_jaxpr/ppermute | solution.py:76
  803.8 30.1 %collective-permute-start.4 = (f32[2,384,1,256]{3,1,0,2:T(8,128)}, f32[2,384,1,256]{3,1,0,2:T(8,128)}, u32[]{:S(2)}, u32[]{:S(2)}) collective-permute-start(f32[2,384,1,256]{3,1,0,2:T(8,128)} %get-tuple-element.662), channel_id=1, source_target_pairs={{0,1},{1,2},{2,3},{3,4},{4,5},{5,6},{6,7},{7,8},{8,9},{9,10},{10,1... | collective-permute-start | bytes 2359304 | tf_op jit(solution)/shard_map/while/body/eval_jaxpr/ppermute | solution.py:75
  803.8 30.1 %collective-permute-start.5 = (f32[2,384,1,256]{3,1,0,2:T(8,128)}, f32[2,384,1,256]{3,1,0,2:T(8,128)}, u32[]{:S(2)}, u32[]{:S(2)}) collective-permute-start(f32[2,384,1,256]{3,1,0,2:T(8,128)} %get-tuple-element.663), channel_id=1, source_target_pairs={{0,1},{1,2},{2,3},{3,4},{4,5},{5,6},{6,7},{7,8},{8,9},{9,10},{10,1... | collective-permute-start | bytes 2359304 | tf_op jit(solution)/shard_map/while/body/eval_jaxpr/ppermute | solution.py:76
  849.5 30.1 %collective-permute-start.4 = (f32[2,384,1,256]{3,1,0,2:T(8,128)}, f32[2,384,1,256]{3,1,0,2:T(8,128)}, u32[]{:S(2)}, u32[]{:S(2)}) collective-permute-start(f32[2,384,1,256]{3,1,0,2:T(8,128)} %get-tuple-element.662), channel_id=1, source_target_pairs={{0,1},{1,2},{2,3},{3,4},{4,5},{5,6},{6,7},{7,8},{8,9},{9,10},{10,1... | collective-permute-start | bytes 2359304 | tf_op jit(solution)/shard_map/while/body/eval_jaxpr/ppermute | solution.py:75
  895.2 30.1 %collective-permute-start.4 = (f32[2,384,1,256]{3,1,0,2:T(8,128)}, f32[2,384,1,256]{3,1,0,2:T(8,128)}, u32[]{:S(2)}, u32[]{:S(2)}) collective-permute-start(f32[2,384,1,256]{3,1,0,2:T(8,128)} %get-tuple-element.662), channel_id=1, source_target_pairs={{0,1},{1,2},{2,3},{3,4},{4,5},{5,6},{6,7},{7,8},{8,9},{9,10},{10,1... | collective-permute-start | bytes 2359304 | tf_op jit(solution)/shard_map/while/body/eval_jaxpr/ppermute | solution.py:75
  895.2 30.1 %collective-permute-start.5 = (f32[2,384,1,256]{3,1,0,2:T(8,128)}, f32[2,384,1,256]{3,1,0,2:T(8,128)}, u32[]{:S(2)}, u32[]{:S(2)}) collective-permute-start(f32[2,384,1,256]{3,1,0,2:T(8,128)} %get-tuple-element.663), channel_id=1, source_target_pairs={{0,1},{1,2},{2,3},{3,4},{4,5},{5,6},{6,7},{7,8},{8,9},{9,10},{10,1... | collective-permute-start | bytes 2359304 | tf_op jit(solution)/shard_map/while/body/eval_jaxpr/ppermute | solution.py:76
  940.9 30.1 %collective-permute-start.4 = (f32[2,384,1,256]{3,1,0,2:T(8,128)}, f32[2,384,1,256]{3,1,0,2:T(8,128)}, u32[]{:S(2)}, u32[]{:S(2)}) collective-permute-start(f32[2,384,1,256]{3,1,0,2:T(8,128)} %get-tuple-element.662), channel_id=1, source_target_pairs={{0,1},{1,2},{2,3},{3,4},{4,5},{5,6},{6,7},{7,8},{8,9},{9,10},{10,1... | collective-permute-start | bytes 2359304 | tf_op jit(solution)/shard_map/while/body/eval_jaxpr/ppermute | solution.py:75
  986.6 30.1 %collective-permute-start.4 = (f32[2,384,1,256]{3,1,0,2:T(8,128)}, f32[2,384,1,256]{3,1,0,2:T(8,128)}, u32[]{:S(2)}, u32[]{:S(2)}) collective-permute-start(f32[2,384,1,256]{3,1,0,2:T(8,128)} %get-tuple-element.662), channel_id=1, source_target_pairs={{0,1},{1,2},{2,3},{3,4},{4,5},{5,6},{6,7},{7,8},{8,9},{9,10},{10,1... | collective-permute-start | bytes 2359304 | tf_op jit(solution)/shard_map/while/body/eval_jaxpr/ppermute | solution.py:75
  (223 other events, 1606.4 us)
where the time goes:
time: 1040 us
  waiting for transfers between devices  580 us (56%)
  matrix products  229 us (22%)
  local copies, waits for them, and re-layouts  195 us (19%)
  other arithmetic  25.8 us (2%)
    ppermute x15, waiting for transfers between devices, backward_body(): key_cur = lax.ppermute(key_cur, 'cp', shift_pairs)  352 us
    while x150, local copies, waits for them, and re-layouts  147 us
    ppermute x15, waiting for transfers between devices, forward_body(): key_cur = lax.ppermute(key_cur, 'cp', shift_pairs)  108 us
    ppermute x15, waiting for transfers between devices, forward_body(): value_cur = lax.ppermute(value_cur, 'cp', shift_pairs)  63.2 us
    ppermute x15, waiting for transfers between devices, backward_body(): value_cur = lax.ppermute(value_cur, 'cp', shift_pairs)  51.5 us
    dot_general x15, matrix products, backward_step(): jnp.einsum('bgrqk,bqgrd->bkgd', grad_score, query5, preferred_element_typ...  48.8 us
    dot_general x15, matrix products, backward_step(): jnp.einsum('bgrqk,bqgrd->bkgd', prob_low, grad5, preferred_element_type=j...  45.4 us
    dot_general x29, matrix products, block_scores(): jnp.einsum('bqgrd,bkgd->bgrqk', query5, key_blk, preferred_element_type=j...  39.3 us
  transfers between devices with their start and end apart: 92, of which 62 were waited for; matrix products, arithmetic and copies ran while one was open for 4% of the time, Pallas kernels for 0%

commit v1 on v0

v1 whole, which is shorter than its diff:
```python
import functools

import jax
import jax.numpy as jnp
from jax import lax
from jax.experimental import pallas as pl
from jax.experimental.pallas import tpu as pltpu
from jax.sharding import PartitionSpec as P

MESH = pl.DeviceIdType.MESH
LOG2E = 1.4426950408889634
LN2 = 0.6931471805599453
TILE = 256


def attention_kernel(n, scale, q_hbm, k_hbm, v_hbm, g_hbm, out_hbm, lse_hbm, dq_hbm, dk_hbm, dv_hbm,
                     k_all, v_all, turned, q_s, q_t, g_s, g_t, acc, run_m, run_l, delta, lse_s, out_s, dq_s, dk_s, dv_s,
                     dk_sum, dv_sum, dk_dn, dv_dn, dk_up, dv_up,
                     load_sem, swap_send, swap_recv, kv_up_send, kv_up_recv, kv_dn_send, kv_dn_recv,
                     dkv_dn_send, dkv_dn_recv, dkv_up_send, dkv_up_recv, store_sem, back_send, back_recv):
    heads, chunk, head_dim = q_s.shape
    half = chunk // 2
    tiles = chunk // TILE
    rank = lax.axis_index("cp")
    chip = rank // 2
    core = rank % 2
    other = 1 - core
    peer = 2 * chip + other
    above = 2 * ((chip + 1) % n) + core
    below = 2 * ((chip + n - 1) % n) + core
    mine = pl.ds(pl.multiple_of(core * half, half), half)
    theirs = pl.ds(pl.multiple_of(other * half, half), half)
    hops_up = (n // 2, n - 1 - n // 2)
    hops_dn = (n - 1 - n // 2, n // 2)
    kv_all = (k_all, v_all)
    sums = (dk_sum, dv_sum)
    from_up = (dk_dn, dv_dn)
    from_dn = (dk_up, dv_up)
    fold = scale * LOG2E

    def remote(src, dst, send_sem, recv_sem, device):
        return pltpu.make_async_remote_copy(src_ref=src, dst_ref=dst, send_sem=send_sem, recv_sem=recv_sem, device_id={"cp": device}, device_id_type=MESH)

    barrier = pltpu.get_barrier_semaphore()
    for device in (peer, above, below):
        pl.semaphore_signal(barrier, inc=1, device_id={"cp": device}, device_id_type=MESH)
    pl.semaphore_wait(barrier, 3)

    places = (k_all.at[chip, mine], v_all.at[chip, mine], q_s.at[:, mine], g_s.at[:, mine])
    sources = (k_hbm, v_hbm, q_hbm, g_hbm)
    swaps = [remote(sources[i].at[other], places[i], swap_send.at[i], swap_recv.at[i], peer) for i in range(4)]
    loads = [pltpu.make_async_copy(sources[i].at[core], places[i], load_sem.at[i]) for i in range(4)]
    for i in range(4):
        swaps[i].start()
        loads[i].start()

    def arrived(i):
        loads[i].wait()
        swaps[i].wait_recv()

    def kv_up(a, step, j):
        return remote(kv_all[a].at[j], kv_all[a].at[j], kv_up_send.at[a, step], kv_up_recv.at[a, step], above)

    def kv_dn(a, step, j):
        return remote(kv_all[a].at[j], kv_all[a].at[j], kv_dn_send.at[a, step], kv_dn_recv.at[a, step], below)

    def sends_up(a, step):
        return (chip < n - 1) & (chip - step >= 0) & (step < hops_up[a])

    def sends_dn(a, step):
        return ((chip + step) % n < hops_dn[a]) & (step < hops_dn[a])

    for a in range(2):
        arrived(a)

        @pl.when(sends_up(a, 0))
        def _():
            kv_up(a, 0, chip).start()

        @pl.when(sends_dn(a, 0))
        def _():
            kv_dn(a, 0, chip).start()

    def take_up(a, step):
        j = chip - 1 - step

        @pl.when((j >= 0) & (step < hops_up[a]))
        def _():
            kv_up(a, step, j).wait_recv()

            @pl.when(sends_up(a, step + 1))
            def _():
                kv_up(a, step + 1, j).start()

    def take_dn(a, step):
        j = (chip + 1 + step) % n

        @pl.when((j < hops_dn[a]) & (step < hops_dn[a]))
        def _():
            kv_dn(a, step, j).wait_recv()

            @pl.when(sends_dn(a, step + 1))
            def _():
                kv_dn(a, step + 1, j).start()

    def turn(ref, j):
        for i in range(tiles):
            turned[:, i * TILE:(i + 1) * TILE] = ref[j, i * TILE:(i + 1) * TILE, :].T

    def causal(rows, i):
        key = lax.broadcasted_iota(jnp.int32, (rows, TILE), 0)
        query = lax.broadcasted_iota(jnp.int32, (rows, TILE), 1) + i * TILE
        return key <= query

    def forward_chunk(j, diagonal):
        turn(v_all, j)

        def head(h, _):
            for i in range(tiles):
                cols = slice(i * TILE, (i + 1) * TILE)
                rows = (i + 1) * TILE if diagonal else chunk
                s = jnp.dot(k_all[j, :rows, :], q_t[h, :, cols], preferred_element_type=jnp.float32) * fold
                if diagonal:
                    s = jnp.where(causal(rows, i), s, -jnp.inf)
                    top = jnp.max(s, axis=0, keepdims=True)
                else:
                    old = run_m[h, :, cols]
                    top = jnp.maximum(old, jnp.max(s, axis=0, keepdims=True))
                p = jnp.exp2(s - top)
                total = jnp.sum(p, axis=0, keepdims=True)
                part = jnp.dot(turned[:, :rows], p.astype(jnp.bfloat16), preferred_element_type=jnp.float32)
                run_m[h, :, cols] = top
                if diagonal:
                    run_l[h, :, cols] = total
                    acc[h, :, cols] = part
                else:
                    alpha = jnp.exp2(old - top)
                    run_l[h, :, cols] = run_l[h, :, cols] * alpha + total
                    acc[h, :, cols] = acc[h, :, cols] * alpha + part
            return 0

        lax.fori_loop(0, heads, head, 0)

    arrived(2)

    def turn_q(h, _):
        for i in range(tiles):
            cols = slice(i * TILE, (i + 1) * TILE)
            q_t[h, :, cols] = q_s[h, cols, :].T
        return 0

    lax.fori_loop(0, heads, turn_q, 0)
    forward_chunk(chip, True)
    arrived(3)

    def turn_g(h, _):
        for i in range(tiles):
            cols = slice(i * TILE, (i + 1) * TILE)
            g_t[h, :, cols] = g_s[h, cols, :].T
        return 0

    lax.fori_loop(0, heads, turn_g, 0)

    def forward_pos(s, _):
        step = s // 2
        up = s % 2 == 0
        last = s == n - 2

        @pl.when(up)
        def _():
            take_up(0, step)
            take_up(1, step)

        @pl.when(jnp.logical_not(up))
        def _():
            take_dn(0, step)
            take_dn(1, step)

        @pl.when(last)
        def _():
            take_dn(1, step)

        j = jnp.where(up, chip - 1 - step, (chip + 1 + step) % n)
        valid = (j >= 0) & (j < chip) & (up | (j < hops_dn[0]))

        @pl.when(valid)
        def _():
            forward_chunk(j, False)

        return 0

    lax.fori_loop(0, n - 1, forward_pos, 0)

    def finish(h, _):
        for i in range(tiles):
            cols = slice(i * TILE, (i + 1) * TILE)
            total = run_l[h, :, cols]
            out = (acc[h, :, cols] / total).astype(jnp.bfloat16)
            acc[h, :, cols] = jnp.zeros((head_dim, TILE), jnp.float32)
            delta[h, :, cols] = jnp.sum(g_t[h, :, cols].astype(jnp.float32) * out.astype(jnp.float32), axis=0, keepdims=True)
            lse2 = run_m[h, :, cols] + jnp.log2(total)
            run_m[h, :, cols] = lse2
            lse_s[h, :, cols] = lse2 * LN2
            out_s[h, cols, :] = out.T
        return 0

    lax.fori_loop(0, heads, finish, 0)

    def give_back(i, src_mine, src_theirs, dst):
        swap = remote(src_theirs, dst.at[core], back_send.at[i], back_recv.at[i], peer)
        keep = pltpu.make_async_copy(src_mine, dst.at[core], store_sem.at[i])
        swap.start()
        keep.start()
        return swap, keep

    pending = [
        give_back(0, out_s.at[:, mine], out_s.at[:, theirs], out_hbm),
        give_back(1, lse_s.at[:, :, mine], lse_s.at[:, :, theirs], lse_hbm),
    ]

    def backward_chunk(j, diagonal):
        turn(k_all, j)
        dk_sum[j] = jnp.zeros((chunk, head_dim), jnp.float32)
        dv_sum[j] = jnp.zeros((chunk, head_dim), jnp.float32)

        def head(h, _):
            for i in range(tiles):
                cols = slice(i * TILE, (i + 1) * TILE)
                rows = (i + 1) * TILE if diagonal else chunk
                s = jnp.dot(k_all[j, :rows, :], q_t[h, :, cols], preferred_element_type=jnp.float32) * fold
                if diagonal:
                    s = jnp.where(causal(rows, i), s, -jnp.inf)
                p = jnp.exp2(s - run_m[h, :, cols])
                dp = jnp.dot(v_all[j, :rows, :], g_t[h, :, cols], preferred_element_type=jnp.float32)
                ds = (p * (dp - delta[h, :, cols])).astype(jnp.bfloat16)
                dv_sum[j, :rows, :] += jnp.dot(p.astype(jnp.bfloat16), g_s[h, cols, :], preferred_element_type=jnp.float32)
                dk_sum[j, :rows, :] += jnp.dot(ds, q_s[h, cols, :], preferred_element_type=jnp.float32)
                acc[h, :, cols] += jnp.dot(turned[:, :rows], ds, preferred_element_type=jnp.float32)
            return 0

        lax.fori_loop(0, heads, head, 0)

    def sum_dn(a, step, j):
        return remote(sums[a].at[j], from_up[a].at[step], dkv_dn_send.at[a, step], dkv_dn_recv.at[a, step], below)

    def sum_up(a, step, src):
        return remote(src, from_dn[a].at[step], dkv_up_send.at[a, step], dkv_up_recv.at[a, step], above)

    def gives_dn(a, step):
        return (chip - hops_up[a] + step >= 0) & (step < hops_up[a])

    def up_index(a, step):
        return (chip + hops_dn[a] - step + n) % n

    def gives_up(a, step):
        j = up_index(a, step)
        return (j < hops_dn[a]) & (j != chip) & (step < hops_dn[a])

    def add_in(a, j, part):
        sums[a][j] = sums[a][j] + part

    def pass_dn(a, step):
        @pl.when(gives_dn(a, step))
        def _():
            j = chip - hops_up[a] + step

            before = jnp.maximum(step - 1, 0)

            @pl.when((step >= 1) & (chip < n - 1))
            def _():
                sum_dn(a, before, j).wait_recv()
                add_in(a, j, from_up[a][before])

            sum_dn(a, step, j).start()

    def pass_up(a, step):
        @pl.when(gives_up(a, step))
        def _():
            j = up_index(a, step)
            before = jnp.maximum(step - 1, 0)

            @pl.when(step >= 1)
            def _():
                sum_up(a, before, sums[a].at[j]).wait_recv()

            @pl.when(j < chip)
            def _():
                @pl.when(step >= 1)
                def _():
                    add_in(a, j, from_dn[a][before])

                sum_up(a, step, sums[a].at[j]).start()

            @pl.when(j > chip)
            def _():
                sum_up(a, step, from_dn[a].at[before]).start()

    def backward_pos(s, _):
        step = jnp.maximum(s - 1, 0) // 2
        first = s == 0
        down = s % 2 == 1
        near = chip - hops_up[1] + step
        far = up_index(0, step)
        j = jnp.where(first, chip - n // 2, jnp.where(down, near, far))
        valid = (j >= 0) & (j < chip) & (first | down | (j < hops_dn[0]))

        @pl.when(valid)
        def _():
            backward_chunk(j, False)

        @pl.when(first)
        def _():
            pass_dn(0, 0)
            pass_up(1, 0)

        @pl.when(down)
        def _():
            pass_dn(0, step + 1)
            pass_dn(1, step)

        @pl.when(jnp.logical_not(first | down))
        def _():
            pass_up(0, step)
            pass_up(1, step + 1)

        @pl.when(s == n // 2 - 1)
        def _():
            backward_chunk(chip, True)

        return 0

    lax.fori_loop(0, n - 1, backward_pos, 0)

    def finish_q(h, _):
        for i in range(tiles):
            cols = slice(i * TILE, (i + 1) * TILE)
            dq_s[h, cols, :] = (acc[h, :, cols] * scale).astype(jnp.bfloat16).T
        return 0

    lax.fori_loop(0, heads, finish_q, 0)
    pending.append(give_back(2, dq_s.at[:, mine], dq_s.at[:, theirs], dq_hbm))

    for a in range(2):
        @pl.when(chip < hops_dn[a])
        def _():
            sum_up(a, hops_dn[a] - 1, sums[a].at[chip]).wait_recv()
            add_in(a, chip, from_dn[a][hops_dn[a] - 1])

        @pl.when(chip < n - 1)
        def _():
            sum_dn(a, hops_up[a] - 1, chip).wait_recv()
            add_in(a, chip, from_up[a][hops_up[a] - 1])

        if a == 0:
            dk_s[...] = (dk_sum[chip] * scale).astype(jnp.bfloat16)
            pending.append(give_back(3, dk_s.at[mine], dk_s.at[theirs], dk_hbm))
        else:
            dv_s[...] = dv_sum[chip].astype(jnp.bfloat16)
            pending.append(give_back(4, dv_s.at[mine], dv_s.at[theirs], dv_hbm))

    for i in range(4):
        swaps[i].wait_send()
    for a in range(2):
        for step in range(hops_up[a]):
            @pl.when(sends_up(a, step))
            def _():
                kv_up(a, step, 0).wait_send()

            @pl.when(gives_dn(a, step))
            def _():
                sum_dn(a, step, 0).wait_send()

        for step in range(hops_dn[a]):
            @pl.when(sends_dn(a, step))
            def _():
                kv_dn(a, step, 0).wait_send()

            @pl.when(gives_up(a, step))
            def _():
                sum_up(a, step, sums[a].at[0]).wait_send()

    for swap, keep in pending:
        keep.wait()
        swap.wait()


def solution(mesh):
    chips = mesh.shape["cp"] // 2

    def attention_shard(queries, keys, values, out_grad):
        batch, tokens, heads, head_dim = queries.shape
        chunk = 2 * tokens
        half = chips // 2
        bf16, f32 = jnp.bfloat16, jnp.float32
        q = jnp.transpose(queries, (0, 2, 1, 3))
        g = jnp.transpose(out_grad, (0, 2, 1, 3))
        k = keys.reshape(batch, tokens, head_dim)
        v = values.reshape(batch, tokens, head_dim)
        any_spec = pl.BlockSpec(memory_space=pl.ANY)
        dma = pltpu.SemaphoreType.DMA
        out, lse, dq, dk, dv = pl.pallas_call(
            functools.partial(attention_kernel, chips, head_dim ** -0.5),
            out_shape=(
                jax.ShapeDtypeStruct(q.shape, bf16),
                jax.ShapeDtypeStruct((batch, heads, 1, tokens), f32),
                jax.ShapeDtypeStruct(q.shape, bf16),
                jax.ShapeDtypeStruct(k.shape, bf16),
                jax.ShapeDtypeStruct(k.shape, bf16),
            ),
            in_specs=[any_spec] * 4,
            out_specs=(any_spec,) * 5,
            scratch_shapes=[
                pltpu.VMEM((chips, chunk, head_dim), bf16),
                pltpu.VMEM((chips, chunk, head_dim), bf16),
                pltpu.VMEM((head_dim, chunk), bf16),
                pltpu.VMEM((heads, chunk, head_dim), bf16),
                pltpu.VMEM((heads, head_dim, chunk), bf16),
                pltpu.VMEM((heads, chunk, head_dim), bf16),
                pltpu.VMEM((heads, head_dim, chunk), bf16),
                pltpu.VMEM((heads, head_dim, chunk), f32),
                pltpu.VMEM((heads, 1, chunk), f32),
                pltpu.VMEM((heads, 1, chunk), f32),
                pltpu.VMEM((heads, 1, chunk), f32),
                pltpu.VMEM((heads, 1, chunk), f32),
                pltpu.VMEM((heads, chunk, head_dim), bf16),
                pltpu.VMEM((heads, chunk, head_dim), bf16),
                pltpu.VMEM((chunk, head_dim), bf16),
                pltpu.VMEM((chunk, head_dim), bf16),
                pltpu.VMEM((chips, chunk, head_dim), f32),
                pltpu.VMEM((chips, chunk, head_dim), f32),
                pltpu.VMEM((half, chunk, head_dim), f32),
                pltpu.VMEM((half - 1, chunk, head_dim), f32),
                pltpu.VMEM((half - 1, chunk, head_dim), f32),
                pltpu.VMEM((half, chunk, head_dim), f32),
                dma((4,)), dma((4,)), dma((4,)),
                dma((2, half)), dma((2, half)), dma((2, half)), dma((2, half)),
                dma((2, half)), dma((2, half)), dma((2, half)), dma((2, half)),
                dma((5,)), dma((5,)), dma((5,)),
            ],
            compiler_params=pltpu.CompilerParams(collective_id=0, has_side_effects=True, vmem_limit_bytes=67043328),
            name="ring_attention",
        )(q, k, v, g)
        back = (0, 2, 1, 3)
        return (
            jnp.transpose(out, back),
            lse.reshape(batch, heads, tokens),
            jnp.transpose(dq, back),
            dk.reshape(keys.shape),
            dv.reshape(values.shape),
        )

    seq_spec = P("dp", "cp")
    return jax.shard_map(attention_shard, mesh=mesh, in_specs=(seq_spec,) * 4, out_specs=(seq_spec, P("dp", None, "cp"), seq_spec, seq_spec, seq_spec), check_vma=False)
```

time: 1040 us -> 223 us (0.21)
  the two profiles are of different devices: /device:TPU:254 before, /device:TPU:21 now
where the time goes in v1:
time: 223 us; the launch traced here: 222 us
  Pallas kernels  209 us (94%)
  local copies, waits for them, and re-layouts  12.4 us (6%)
    pallas_call x1, Pallas kernels, attention_shard(): pl.pallas_call(functools.partial(attention_kernel, chips, head_dim ** (-0...  209 us
    unnamed x13, local copies, waits for them, and re-layouts  8.35 us

profile of v1, /device:TPU:21, one launch (start us, length us, event | category | flops | bytes accessed | tf_op | source)
XLA Modules:
  0.0 222.1 jit_solution(315999263854444576)
XLA Ops:
  0.6 4.1 %copy_bitcast_fusion = (bf16[2,4,384,256]{3,2,1,0:T(8,128)(2,1)}, bf16[2,4,384,256]{3,2,1,0:T(8,128)(2,1)}) fusion(bf16[2,384,4,256]{3,2,1,0:T(4,128)(2,1)} %param.7, bf16[2,384,4,256]{3,2,1,0:T(4,128)(2,1)} %param.4), kind=kLoop, calls=%fused_computation | loop fusion | bytes 6291456 | tf_op jit(solution)/shard_map/transpose | solution.py:396
  4.7 209.0 %ring_attention.1 = (bf16[2,4,384,256]{3,2,1,0:T(8,128)(2,1)}, f32[2,4,1,384]{3,2,1,0:T(1,128)}, bf16[2,4,384,256]{3,2,1,0:T(8,128)(2,1)}, bf16[2,384,256]{2,1,0:T(8,128)(2,1)}, bf16[2,384,256]{2,1,0:T(8,128)(2,1)}) custom-call(bf16[2,4,384,256]{3,2,1,0:T(8,128)(2,1)} %get-tuple-element.21.q_hbm, bf16[2,384,256]{2,1,0:T(8,128)(2,1)} %bitcast.21, ...), custom_call_target="tpu_custom_call" | custom-call | tf_op jit(solution)/shard_map/ring_attention/pallas_call | solution.py:401
  213.8 0.0 copy-start.3
  213.8 0.0 copy-start
  213.8 3.9 %copy.11 = bf16[2,384,4,256]{3,2,1,0:T(4,128)(2,1)} copy(bf16[2,384,4,256]{3,1,2,0:T(8,128)(2,1)} %bitcast.18) | data formatting | bytes 3145728
  217.7 0.0 copy-done.3
  217.7 0.6 copy.19
  218.3 0.0 copy-done
  218.3 0.0 copy-start.2
  218.3 0.0 copy-start.1
  218.3 2.4 %copy.12 = bf16[2,384,4,256]{3,2,1,0:T(4,128)(2,1)} copy(bf16[2,384,4,256]{3,1,2,0:T(8,128)(2,1)S(1)} %bitcast.17) | data formatting | bytes 3145728
  220.6 0.0 copy-done.2
  220.6 0.7 copy.22
  221.4 0.0 copy-done.1
  221.4 0.7 copy.23
Async XLA Ops:
  213.8 3.9 %copy-start.3 = (f32[2,4,1,384]{3,2,1,0:T(1,128)S(1)}, f32[2,4,1,384]{3,2,1,0:T(1,128)}, u32[]{:S(2)}) copy-start(f32[2,4,1,384]{3,2,1,0:T(1,128)} %get-tuple-element.11) | copy-start | bytes 36868
  213.8 4.5 %copy-start = (bf16[2,4,384,256]{3,2,1,0:T(8,128)(2,1)S(1)}, bf16[2,4,384,256]{3,2,1,0:T(8,128)(2,1)}, u32[]{:S(2)}) copy-start(bf16[2,4,384,256]{3,2,1,0:T(8,128)(2,1)} %get-tuple-element.12) | copy-start | bytes 4718596
  218.3 2.4 %copy-start.2 = (bf16[2,384,256]{2,1,0:T(8,128)(2,1)S(1)}, bf16[2,384,256]{2,1,0:T(8,128)(2,1)}, u32[]{:S(2)}) copy-start(bf16[2,384,256]{2,1,0:T(8,128)(2,1)} %get-tuple-element.13) | copy-start | bytes 1179652
  218.3 3.1 %copy-start.1 = (bf16[2,384,256]{2,1,0:T(8,128)(2,1)S(1)}, bf16[2,384,256]{2,1,0:T(8,128)(2,1)}, u32[]{:S(2)}) copy-start(bf16[2,384,256]{2,1,0:T(8,128)(2,1)} %get-tuple-element.14) | copy-start | bytes 1179652

commit v2 on v1

--- a/solution.py
+++ b/solution.py
@@ -17,7 +17,7 @@
                      k_all, v_all, turned, q_s, q_t, g_s, g_t, acc, run_m, run_l, delta, lse_s, out_s, dq_s, dk_s, dv_s,
                      dk_sum, dv_sum, dk_dn, dv_dn, dk_up, dv_up,
                      load_sem, swap_send, swap_recv, kv_up_send, kv_up_recv, kv_dn_send, kv_dn_recv,
-                     dkv_dn_send, dkv_dn_recv, dkv_up_send, dkv_up_recv, store_sem, back_send, back_recv):
+                     dkv_dn_send, dkv_dn_recv, dkv_up_send, dkv_up_recv, store_sem, back_send, back_recv, go_sem):
     heads, chunk, head_dim = q_s.shape
     half = chunk // 2
     tiles = chunk // TILE
@@ -70,16 +70,33 @@
     def sends_dn(a, step):
         return ((chip + step) % n < hops_dn[a]) & (step < hops_dn[a])
 
+    def send_own(a):
+        @pl.when(sends_up(a, 0))
+        def _():
+            kv_up(a, 0, chip).start()
+
+        @pl.when(sends_dn(a, 0))
+        def _():
+            kv_dn(a, 0, chip).start()
+
+    def sent_all():
+        for a in range(2):
+            for step in range(hops_up[a]):
+                @pl.when(sends_up(a, step))
+                def _():
+                    kv_up(a, step, 0).wait_send()
+
+            for step in range(hops_dn[a]):
+                @pl.when(sends_dn(a, step))
+                def _():
+                    kv_dn(a, step, 0).wait_send()
+
     for a in range(2):
         arrived(a)
 
-        @pl.when(sends_up(a, 0))
-        def _():
-            kv_up(a, 0, chip).start()
-
-        @pl.when(sends_dn(a, 0))
-        def _():
-            kv_dn(a, 0, chip).start()
+        @pl.when(core == 0)
+        def _():
+            send_own(a)
 
     def take_up(a, step):
         j = chip - 1 - step
@@ -161,6 +178,12 @@
 
     lax.fori_loop(0, heads, turn_g, 0)
 
+    @pl.when(core == 1)
+    def _():
+        pl.semaphore_wait(go_sem, 1)
+        send_own(0)
+        send_own(1)
+
     def forward_pos(s, _):
         step = s // 2
         up = s % 2 == 0
@@ -179,6 +202,11 @@
         @pl.when(last)
         def _():
             take_dn(1, step)
+            sent_all()
+
+            @pl.when(core == 0)
+            def _():
+                pl.semaphore_signal(go_sem, inc=1, device_id={"cp": peer}, device_id_type=MESH)
 
         j = jnp.where(up, chip - 1 - step, (chip + 1 + step) % n)
         valid = (j >= 0) & (j < chip) & (up | (j < hops_dn[0]))
@@ -246,15 +274,25 @@
     def sum_up(a, step, src):
         return remote(src, from_dn[a].at[step], dkv_up_send.at[a, step], dkv_up_recv.at[a, step], above)
 
+    wide = n // 2
+
     def gives_dn(a, step):
-        return (chip - hops_up[a] + step >= 0) & (step < hops_up[a])
-
-    def up_index(a, step):
-        return (chip + hops_dn[a] - step + n) % n
+        skip = (a == 0) & (step == 0) & (chip == n - 1)
+        return (chip - hops_up[a] + step >= 0) & (step < hops_up[a]) & jnp.logical_not(skip)
+
+    def gets_dn(a, step):
+        skip = (a == 0) & (step == 1) & (chip == n - 2)
+        return (step >= 1) & (chip < n - 1) & jnp.logical_not(skip)
+
+    def up_index(step):
+        return (chip + wide - step + n) % n
 
     def gives_up(a, step):
-        j = up_index(a, step)
-        return (j < hops_dn[a]) & (j != chip) & (step < hops_dn[a])
+        j = up_index(step)
+        return (j < wide) & (j != chip) & (step < wide) & ((a == 1) | (step >= 1) | (chip == n - 1))
+
+    def gets_up(a, step):
+        return (step >= 2 - a) | ((step >= 1) & (up_index(step) > chip))
 
     def add_in(a, j, part):
         sums[a][j] = sums[a][j] + part
@@ -266,7 +304,7 @@
 
             before = jnp.maximum(step - 1, 0)
 
-            @pl.when((step >= 1) & (chip < n - 1))
+            @pl.when(gets_dn(a, step))
             def _():
                 sum_dn(a, before, j).wait_recv()
                 add_in(a, j, from_up[a][before])
@@ -276,16 +314,16 @@
     def pass_up(a, step):
         @pl.when(gives_up(a, step))
         def _():
-            j = up_index(a, step)
+            j = up_index(step)
             before = jnp.maximum(step - 1, 0)
 
-            @pl.when(step >= 1)
+            @pl.when(gets_up(a, step))
             def _():
                 sum_up(a, before, sums[a].at[j]).wait_recv()
 
             @pl.when(j < chip)
             def _():
-                @pl.when(step >= 1)
+                @pl.when(gets_up(a, step))
                 def _():
                     add_in(a, j, from_dn[a][before])
 
@@ -300,9 +338,9 @@
         first = s == 0
         down = s % 2 == 1
         near = chip - hops_up[1] + step
-        far = up_index(0, step)
+        far = up_index(step + 1)
         j = jnp.where(first, chip - n // 2, jnp.where(down, near, far))
-        valid = (j >= 0) & (j < chip) & (first | down | (j < hops_dn[0]))
+        valid = (j >= 0) & (j < chip) & (first | down | (j < wide))
 
         @pl.when(valid)
         def _():
@@ -311,6 +349,7 @@
         @pl.when(first)
         def _():
             pass_dn(0, 0)
+            pass_up(0, 0)
             pass_up(1, 0)
 
         @pl.when(down)
@@ -320,7 +359,7 @@
 
         @pl.when(jnp.logical_not(first | down))
         def _():
-            pass_up(0, step)
+            pass_up(0, step + 1)
             pass_up(1, step + 1)
 
         @pl.when(s == n // 2 - 1)
@@ -341,10 +380,10 @@
     pending.append(give_back(2, dq_s.at[:, mine], dq_s.at[:, theirs], dq_hbm))
 
     for a in range(2):
-        @pl.when(chip < hops_dn[a])
-        def _():
-            sum_up(a, hops_dn[a] - 1, sums[a].at[chip]).wait_recv()
-            add_in(a, chip, from_dn[a][hops_dn[a] - 1])
+        @pl.when(chip < wide)
+        def _():
+            sum_up(a, wide - 1, sums[a].at[chip]).wait_recv()
+            add_in(a, chip, from_dn[a][wide - 1])
 
         @pl.when(chip < n - 1)
         def _():
@@ -362,19 +401,11 @@
         swaps[i].wait_send()
     for a in range(2):
         for step in range(hops_up[a]):
-            @pl.when(sends_up(a, step))
-            def _():
-                kv_up(a, step, 0).wait_send()
-
             @pl.when(gives_dn(a, step))
             def _():
                 sum_dn(a, step, 0).wait_send()
 
-        for step in range(hops_dn[a]):
-            @pl.when(sends_dn(a, step))
-            def _():
-                kv_dn(a, step, 0).wait_send()
-
+        for step in range(wide):
             @pl.when(gives_up(a, step))
             def _():
                 sum_up(a, step, sums[a].at[0]).wait_send()
@@ -430,12 +461,12 @@
                 pltpu.VMEM((chips, chunk, head_dim), f32),
                 pltpu.VMEM((half, chunk, head_dim), f32),
                 pltpu.VMEM((half - 1, chunk, head_dim), f32),
-                pltpu.VMEM((half - 1, chunk, head_dim), f32),
+                pltpu.VMEM((half, chunk, head_dim), f32),
                 pltpu.VMEM((half, chunk, head_dim), f32),
                 dma((4,)), dma((4,)), dma((4,)),
                 dma((2, half)), dma((2, half)), dma((2, half)), dma((2, half)),
                 dma((2, half)), dma((2, half)), dma((2, half)), dma((2, half)),
-                dma((5,)), dma((5,)), dma((5,)),
+                dma((5,)), dma((5,)), dma((5,)), pltpu.SemaphoreType.REGULAR,
             ],
             compiler_params=pltpu.CompilerParams(collective_id=0, has_side_effects=True, vmem_limit_bytes=67043328),
             name="ring_attention",

time: 223 us -> 227 us (1.018)
  Pallas kernels: 209 us -> 214 us
    pallas_call x1, Pallas kernels: 209 us -> 214 us  [attention_shard(): pl.pallas_call(functools.partial(attention_kernel, chips, head_dim ** (-0...]
where the time goes in v2:
time: 227 us
  Pallas kernels  214 us (94%)
  local copies, waits for them, and re-layouts  12.4 us (5%)
    pallas_call x1, Pallas kernels, attention_shard(): pl.pallas_call(functools.partial(attention_kernel, chips, head_dim ** (-0...  214 us
    unnamed x13, local copies, waits for them, and re-layouts  8.35 us

profile of v2, /device:TPU:21, one launch (start us, length us, event | category | flops | bytes accessed | tf_op | source)
XLA Modules:
  0.0 226.9 jit_solution(18990493634569808)
XLA Ops:
  0.6 4.1 %copy_bitcast_fusion = (bf16[2,4,384,256]{3,2,1,0:T(8,128)(2,1)}, bf16[2,4,384,256]{3,2,1,0:T(8,128)(2,1)}) fusion(bf16[2,384,4,256]{3,2,1,0:T(4,128)(2,1)} %param.7, bf16[2,384,4,256]{3,2,1,0:T(4,128)(2,1)} %param.4), kind=kLoop, calls=%fused_computation | loop fusion | bytes 6291456 | tf_op jit(solution)/shard_map/transpose | solution.py:427
  4.7 213.8 %ring_attention.1 = (bf16[2,4,384,256]{3,2,1,0:T(8,128)(2,1)}, f32[2,4,1,384]{3,2,1,0:T(1,128)}, bf16[2,4,384,256]{3,2,1,0:T(8,128)(2,1)}, bf16[2,384,256]{2,1,0:T(8,128)(2,1)}, bf16[2,384,256]{2,1,0:T(8,128)(2,1)}) custom-call(bf16[2,4,384,256]{3,2,1,0:T(8,128)(2,1)} %get-tuple-element.21.q_hbm, bf16[2,384,256]{2,1,0:T(8,128)(2,1)} %bitcast.21, ...), custom_call_target="tpu_custom_call" | custom-call | tf_op jit(solution)/shard_map/ring_attention/pallas_call | solution.py:432
  218.5 0.0 copy-start.3
  218.5 0.0 copy-start
  218.5 3.9 %copy.11 = bf16[2,384,4,256]{3,2,1,0:T(4,128)(2,1)} copy(bf16[2,384,4,256]{3,1,2,0:T(8,128)(2,1)} %bitcast.18) | data formatting | bytes 3145728
  222.4 0.0 copy-done.3
  222.4 0.6 copy.19
  223.0 0.0 copy-done
  223.0 0.0 copy-start.2
  223.0 0.0 copy-start.1
  223.0 2.4 %copy.12 = bf16[2,384,4,256]{3,2,1,0:T(4,128)(2,1)} copy(bf16[2,384,4,256]{3,1,2,0:T(8,128)(2,1)S(1)} %bitcast.17) | data formatting | bytes 3145728
  225.4 0.0 copy-done.2
  225.4 0.7 copy.22
  226.1 0.0 copy-done.1
  226.1 0.7 copy.23
Async XLA Ops:
  218.5 3.9 %copy-start.3 = (f32[2,4,1,384]{3,2,1,0:T(1,128)S(1)}, f32[2,4,1,384]{3,2,1,0:T(1,128)}, u32[]{:S(2)}) copy-start(f32[2,4,1,384]{3,2,1,0:T(1,128)} %get-tuple-element.11) | copy-start | bytes 36868
  218.5 4.5 %copy-start = (bf16[2,4,384,256]{3,2,1,0:T(8,128)(2,1)S(1)}, bf16[2,4,384,256]{3,2,1,0:T(8,128)(2,1)}, u32[]{:S(2)}) copy-start(bf16[2,4,384,256]{3,2,1,0:T(8,128)(2,1)} %get-tuple-element.12) | copy-start | bytes 4718596
  223.0 2.4 %copy-start.2 = (bf16[2,384,256]{2,1,0:T(8,128)(2,1)S(1)}, bf16[2,384,256]{2,1,0:T(8,128)(2,1)}, u32[]{:S(2)}) copy-start(bf16[2,384,256]{2,1,0:T(8,128)(2,1)} %get-tuple-element.13) | copy-start | bytes 1179652
  223.0 3.1 %copy-start.1 = (bf16[2,384,256]{2,1,0:T(8,128)(2,1)S(1)}, bf16[2,384,256]{2,1,0:T(8,128)(2,1)}, u32[]{:S(2)}) copy-start(bf16[2,384,256]{2,1,0:T(8,128)(2,1)} %get-tuple-element.14) | copy-start | bytes 1179652

commit v3 on v2

--- a/solution.py
+++ b/solution.py
@@ -17,7 +17,7 @@
                      k_all, v_all, turned, q_s, q_t, g_s, g_t, acc, run_m, run_l, delta, lse_s, out_s, dq_s, dk_s, dv_s,
                      dk_sum, dv_sum, dk_dn, dv_dn, dk_up, dv_up,
                      load_sem, swap_send, swap_recv, kv_up_send, kv_up_recv, kv_dn_send, kv_dn_recv,
-                     dkv_dn_send, dkv_dn_recv, dkv_up_send, dkv_up_recv, store_sem, back_send, back_recv, go_sem):
+                     dkv_dn_send, dkv_dn_recv, dkv_up_send, dkv_up_recv, store_sem, back_send, back_recv):
     heads, chunk, head_dim = q_s.shape
     half = chunk // 2
     tiles = chunk // TILE
@@ -70,33 +70,19 @@
     def sends_dn(a, step):
         return ((chip + step) % n < hops_dn[a]) & (step < hops_dn[a])
 
-    def send_own(a):
+    def own_up(a):
         @pl.when(sends_up(a, 0))
         def _():
             kv_up(a, 0, chip).start()
 
+    def own_dn(a):
         @pl.when(sends_dn(a, 0))
         def _():
             kv_dn(a, 0, chip).start()
 
-    def sent_all():
-        for a in range(2):
-            for step in range(hops_up[a]):
-                @pl.when(sends_up(a, step))
-                def _():
-                    kv_up(a, step, 0).wait_send()
-
-            for step in range(hops_dn[a]):
-                @pl.when(sends_dn(a, step))
-                def _():
-                    kv_dn(a, step, 0).wait_send()
-
-    for a in range(2):
-        arrived(a)
-
-        @pl.when(core == 0)
-        def _():
-            send_own(a)
+    arrived(0)
+    own_up(0)
+    own_dn(0)
 
     def take_up(a, step):
         j = chip - 1 - step
@@ -129,31 +115,60 @@
         query = lax.broadcasted_iota(jnp.int32, (rows, TILE), 1) + i * TILE
         return key <= query
 
-    def forward_chunk(j, diagonal):
-        turn(v_all, j)
-
+    def scores(j, h, i, diagonal):
+        cols = slice(i * TILE, (i + 1) * TILE)
+        rows = (i + 1) * TILE if diagonal else chunk
+        s = jnp.dot(k_all[j, :rows, :], q_t[h, :, cols], preferred_element_type=jnp.float32) * fold
+        if diagonal:
+            s = jnp.where(causal(rows, i), s, -jnp.inf)
+        return cols, rows, s
+
+    def stat_chunk(j, diagonal):
         def head(h, _):
             for i in range(tiles):
-                cols = slice(i * TILE, (i + 1) * TILE)
-                rows = (i + 1) * TILE if diagonal else chunk
-                s = jnp.dot(k_all[j, :rows, :], q_t[h, :, cols], preferred_element_type=jnp.float32) * fold
+                cols, rows, s = scores(j, h, i, diagonal)
+                top = jnp.max(s, axis=0, keepdims=True)
                 if diagonal:
-                    s = jnp.where(causal(rows, i), s, -jnp.inf)
-                    top = jnp.max(s, axis=0, keepdims=True)
+                    run_l[h, :, cols] = jnp.sum(jnp.exp2(s - top), axis=0, keepdims=True)
                 else:
                     old = run_m[h, :, cols]
-                    top = jnp.maximum(old, jnp.max(s, axis=0, keepdims=True))
-                p = jnp.exp2(s - top)
-                total = jnp.sum(p, axis=0, keepdims=True)
-                part = jnp.dot(turned[:, :rows], p.astype(jnp.bfloat16), preferred_element_type=jnp.float32)
+                    top = jnp.maximum(old, top)
+                    run_l[h, :, cols] = run_l[h, :, cols] * jnp.exp2(old - top) + jnp.sum(jnp.exp2(s - top), axis=0, keepdims=True)
                 run_m[h, :, cols] = top
-                if diagonal:
-                    run_l[h, :, cols] = total
-                    acc[h, :, cols] = part
-                else:
-                    alpha = jnp.exp2(old - top)
-                    run_l[h, :, cols] = run_l[h, :, cols] * alpha + total
-                    acc[h, :, cols] = acc[h, :, cols] * alpha + part
+            return 0
+
+        lax.fori_loop(0, heads, head, 0)
+
+    def value_chunk(j, diagonal, grad, output):
+        if output:
+            turn(v_all, j)
+        if grad:
+            dv_sum[j] = jnp.zeros((chunk, head_dim), jnp.float32)
+
+        def head(h, _):
+            for i in range(tiles):
+                cols, rows, s = scores(j, h, i, diagonal)
+                p = jnp.exp2(s - run_m[h, :, cols]).astype(jnp.bfloat16)
+                if grad:
+                    dv_sum[j, :rows, :] += jnp.dot(p, g_s[h, cols, :], preferred_element_type=jnp.float32)
+                if output:
+                    acc[h, :, cols] += jnp.dot(turned[:, :rows], p, preferred_element_type=jnp.float32)
+            return 0
+
+        lax.fori_loop(0, heads, head, 0)
+
+    def key_chunk(j, diagonal):
+        turn(k_all, j)
+        dk_sum[j] = jnp.zeros((chunk, head_dim), jnp.float32)
+
+        def head(h, _):
+            for i in range(tiles):
+                cols, rows, s = scores(j, h, i, diagonal)
+                p = jnp.exp2(s - run_m[h, :, cols])
+                dp = jnp.dot(v_all[j, :rows, :], g_t[h, :, cols], preferred_element_type=jnp.float32)
+                ds = (p * (dp - delta[h, :, cols])).astype(jnp.bfloat16)
+                dk_sum[j, :rows, :] += jnp.dot(ds, q_s[h, cols, :], preferred_element_type=jnp.float32)
+                acc[h, :, cols] += jnp.dot(turned[:, :rows], ds, preferred_element_type=jnp.float32)
             return 0
 
         lax.fori_loop(0, heads, head, 0)
@@ -167,106 +182,53 @@
         return 0
 
     lax.fori_loop(0, heads, turn_q, 0)
-    forward_chunk(chip, True)
+    stat_chunk(chip, True)
+    arrived(1)
+
+    def stat_pos(s, _):
+        step = s // 2
+        up = s % 2 == 0
+
+        @pl.when(up)
+        def _():
+            take_up(0, step)
+
+            @pl.when(step == hops_up[0] - 1)
+            def _():
+                own_up(1)
+
+        @pl.when(jnp.logical_not(up))
+        def _():
+            take_dn(0, step)
+
+            @pl.when(step == hops_dn[0] - 1)
+            def _():
+                own_dn(1)
+
+        j = jnp.where(up, chip - 1 - step, (chip + 1 + step) % n)
+        valid = (j >= 0) & (j < chip) & (up | (j < hops_dn[0]))
+
+        @pl.when(valid)
+        def _():
+            stat_chunk(j, False)
+
+        return 0
+
+    lax.fori_loop(0, n - 1, stat_pos, 0)
+
     arrived(3)
 
-    def turn_g(h, _):
+    def finish_stats(h, _):
+        acc[h] = jnp.zeros((head_dim, chunk), jnp.float32)
+        lse2 = run_m[h] + jnp.log2(run_l[h])
+        run_m[h] = lse2
+        lse_s[h] = lse2 * LN2
         for i in range(tiles):
             cols = slice(i * TILE, (i + 1) * TILE)
             g_t[h, :, cols] = g_s[h, cols, :].T
         return 0
 
-    lax.fori_loop(0, heads, turn_g, 0)
-
-    @pl.when(core == 1)
-    def _():
-        pl.semaphore_wait(go_sem, 1)
-        send_own(0)
-        send_own(1)
-
-    def forward_pos(s, _):
-        step = s // 2
-        up = s % 2 == 0
-        last = s == n - 2
-
-        @pl.when(up)
-        def _():
-            take_up(0, step)
-            take_up(1, step)
-
-        @pl.when(jnp.logical_not(up))
-        def _():
-            take_dn(0, step)
-            take_dn(1, step)
-
-        @pl.when(last)
-        def _():
-            take_dn(1, step)
-            sent_all()
-
-            @pl.when(core == 0)
-            def _():
-                pl.semaphore_signal(go_sem, inc=1, device_id={"cp": peer}, device_id_type=MESH)
-
-        j = jnp.where(up, chip - 1 - step, (chip + 1 + step) % n)
-        valid = (j >= 0) & (j < chip) & (up | (j < hops_dn[0]))
-
-        @pl.when(valid)
-        def _():
-            forward_chunk(j, False)
-
-        return 0
-
-    lax.fori_loop(0, n - 1, forward_pos, 0)
-
-    def finish(h, _):
-        for i in range(tiles):
-            cols = slice(i * TILE, (i + 1) * TILE)
-            total = run_l[h, :, cols]
-            out = (acc[h, :, cols] / total).astype(jnp.bfloat16)
-            acc[h, :, cols] = jnp.zeros((head_dim, TILE), jnp.float32)
-            delta[h, :, cols] = jnp.sum(g_t[h, :, cols].astype(jnp.float32) * out.astype(jnp.float32), axis=0, keepdims=True)
-            lse2 = run_m[h, :, cols] + jnp.log2(total)
-            run_m[h, :, cols] = lse2
-            lse_s[h, :, cols] = lse2 * LN2
-            out_s[h, cols, :] = out.T
-        return 0
-
-    lax.fori_loop(0, heads, finish, 0)
-
-    def give_back(i, src_mine, src_theirs, dst):
-        swap = remote(src_theirs, dst.at[core], back_send.at[i], back_recv.at[i], peer)
-        keep = pltpu.make_async_copy(src_mine, dst.at[core], store_sem.at[i])
-        swap.start()
-        keep.start()
-        return swap, keep
-
-    pending = [
-        give_back(0, out_s.at[:, mine], out_s.at[:, theirs], out_hbm),
-        give_back(1, lse_s.at[:, :, mine], lse_s.at[:, :, theirs], lse_hbm),
-    ]
-
-    def backward_chunk(j, diagonal):
-        turn(k_all, j)
-        dk_sum[j] = jnp.zeros((chunk, head_dim), jnp.float32)
-        dv_sum[j] = jnp.zeros((chunk, head_dim), jnp.float32)
-
-        def head(h, _):
-            for i in range(tiles):
-                cols = slice(i * TILE, (i + 1) * TILE)
-                rows = (i + 1) * TILE if diagonal else chunk
-                s = jnp.dot(k_all[j, :rows, :], q_t[h, :, cols], preferred_element_type=jnp.float32) * fold
-                if diagonal:
-                    s = jnp.where(causal(rows, i), s, -jnp.inf)
-                p = jnp.exp2(s - run_m[h, :, cols])
-                dp = jnp.dot(v_all[j, :rows, :], g_t[h, :, cols], preferred_element_type=jnp.float32)
-                ds = (p * (dp - delta[h, :, cols])).astype(jnp.bfloat16)
-                dv_sum[j, :rows, :] += jnp.dot(p.astype(jnp.bfloat16), g_s[h, cols, :], preferred_element_type=jnp.float32)
-                dk_sum[j, :rows, :] += jnp.dot(ds, q_s[h, cols, :], preferred_element_type=jnp.float32)
-                acc[h, :, cols] += jnp.dot(turned[:, :rows], ds, preferred_element_type=jnp.float32)
-            return 0
-
-        lax.fori_loop(0, heads, head, 0)
+    lax.fori_loop(0, heads, finish_stats, 0)
 
     def sum_dn(a, step, j):
         return remote(sums[a].at[j], from_up[a].at[step], dkv_dn_send.at[a, step], dkv_dn_recv.at[a, step], below)
@@ -333,7 +295,7 @@
             def _():
                 sum_up(a, step, from_dn[a].at[before]).start()
 
-    def backward_pos(s, _):
+    def place(s):
         step = jnp.maximum(s - 1, 0) // 2
         first = s == 0
         down = s % 2 == 1
@@ -341,34 +303,108 @@
         far = up_index(step + 1)
         j = jnp.where(first, chip - n // 2, jnp.where(down, near, far))
         valid = (j >= 0) & (j < chip) & (first | down | (j < wide))
+        return step, first, down, j, valid
+
+    early = 3
+
+    def value_pos(s, _):
+        step, first, down, j, valid = place(s)
+
+        @pl.when(down)
+        def _():
+            take_up(1, step)
+            take_dn(1, step)
+
+        @pl.when(valid & (s < early))
+        def _():
+            value_chunk(j, False, True, False)
+
+        @pl.when(valid & (s >= early))
+        def _():
+            value_chunk(j, False, True, True)
+
+        @pl.when(first)
+        def _():
+            pass_up(1, 0)
+
+        @pl.when(down)
+        def _():
+            pass_dn(1, step)
+
+        @pl.when(jnp.logical_not(first | down))
+        def _():
+            pass_up(1, step + 1)
+
+        @pl.when(s == early - 1)
+        def _():
+            value_chunk(chip, True, True, True)
+
+        return 0
+
+    lax.fori_loop(0, n - 1, value_pos, 0)
+    take_dn(1, hops_dn[1] - 1)
+
+    def output_pos(s, _):
+        step, first, down, j, valid = place(early - 1 - s)
 
         @pl.when(valid)
         def _():
-            backward_chunk(j, False)
+            value_chunk(j, False, False, True)
+
+        return 0
+
+    lax.fori_loop(0, early, output_pos, 0)
+
+    def finish(h, _):
+        for i in range(tiles):
+            cols = slice(i * TILE, (i + 1) * TILE)
+            out = acc[h, :, cols].astype(jnp.bfloat16)
+            acc[h, :, cols] = jnp.zeros((head_dim, TILE), jnp.float32)
+            delta[h, :, cols] = jnp.sum(g_t[h, :, cols].astype(jnp.float32) * out.astype(jnp.float32), axis=0, keepdims=True)
+            out_s[h, cols, :] = out.T
+        return 0
+
+    lax.fori_loop(0, heads, finish, 0)
+
+    def give_back(i, src_mine, src_theirs, dst):
+        swap = remote(src_theirs, dst.at[core], back_send.at[i], back_recv.at[i], peer)
+        keep = pltpu.make_async_copy(src_mine, dst.at[core], store_sem.at[i])
+        swap.start()
+        keep.start()
+        return swap, keep
+
+    pending = [
+        give_back(0, out_s.at[:, mine], out_s.at[:, theirs], out_hbm),
+        give_back(1, lse_s.at[:, :, mine], lse_s.at[:, :, theirs], lse_hbm),
+    ]
+
+    def key_pos(s, _):
+        step, first, down, j, valid = place(s)
+
+        @pl.when(valid)
+        def _():
+            key_chunk(j, False)
 
         @pl.when(first)
         def _():
             pass_dn(0, 0)
             pass_up(0, 0)
-            pass_up(1, 0)
 
         @pl.when(down)
         def _():
             pass_dn(0, step + 1)
-            pass_dn(1, step)
 
         @pl.when(jnp.logical_not(first | down))
         def _():
             pass_up(0, step + 1)
-            pass_up(1, step + 1)
 
         @pl.when(s == n // 2 - 1)
         def _():
-            backward_chunk(chip, True)
-
-        return 0
-
-    lax.fori_loop(0, n - 1, backward_pos, 0)
+            key_chunk(chip, True)
+
+        return 0
+
+    lax.fori_loop(0, n - 1, key_pos, 0)
 
     def finish_q(h, _):
         for i in range(tiles):
@@ -401,9 +437,18 @@
         swaps[i].wait_send()
     for a in range(2):
         for step in range(hops_up[a]):
+            @pl.when(sends_up(a, step))
+            def _():
+                kv_up(a, step, 0).wait_send()
+
             @pl.when(gives_dn(a, step))
             def _():
                 sum_dn(a, step, 0).wait_send()
+
+        for step in range(hops_dn[a]):
+            @pl.when(sends_dn(a, step))
+            def _():
+                kv_dn(a, step, 0).wait_send()
 
         for step in range(wide):
             @pl.when(gives_up(a, step))
@@ -466,7 +511,7 @@
                 dma((4,)), dma((4,)), dma((4,)),
                 dma((2, half)), dma((2, half)), dma((2, half)), dma((2, half)),
                 dma((2, half)), dma((2, half)), dma((2, half)), dma((2, half)),
-                dma((5,)), dma((5,)), dma((5,)), pltpu.SemaphoreType.REGULAR,
+                dma((5,)), dma((5,)), dma((5,)),
             ],
             compiler_params=pltpu.CompilerParams(collective_id=0, has_side_effects=True, vmem_limit_bytes=67043328),
             name="ring_attention",

time: 227 us -> 227 us (level)
  no operation moved by 1% of the time
where the time goes in v3:
time: 227 us
  Pallas kernels  214 us (94%)
  local copies, waits for them, and re-layouts  12.4 us (5%)
    pallas_call x1, Pallas kernels, attention_shard(): pl.pallas_call(functools.partial(attention_kernel, chips, head_dim ** (-0...  214 us
    unnamed x13, local copies, waits for them, and re-layouts  8.35 us

profile of v3, /device:TPU:21, one launch (start us, length us, event | category | flops | bytes accessed | tf_op | source)
XLA Modules:
  0.0 226.9 jit_solution(11339014891906487941)
XLA Ops:
  0.6 4.1 %copy_bitcast_fusion = (bf16[2,4,384,256]{3,2,1,0:T(8,128)(2,1)}, bf16[2,4,384,256]{3,2,1,0:T(8,128)(2,1)}) fusion(bf16[2,384,4,256]{3,2,1,0:T(4,128)(2,1)} %param.7, bf16[2,384,4,256]{3,2,1,0:T(4,128)(2,1)} %param.4), kind=kLoop, calls=%fused_computation | loop fusion | bytes 6291456 | tf_op jit(solution)/shard_map/transpose | solution.py:472
  4.7 213.7 %ring_attention.1 = (bf16[2,4,384,256]{3,2,1,0:T(8,128)(2,1)}, f32[2,4,1,384]{3,2,1,0:T(1,128)}, bf16[2,4,384,256]{3,2,1,0:T(8,128)(2,1)}, bf16[2,384,256]{2,1,0:T(8,128)(2,1)}, bf16[2,384,256]{2,1,0:T(8,128)(2,1)}) custom-call(bf16[2,4,384,256]{3,2,1,0:T(8,128)(2,1)} %get-tuple-element.21.q_hbm, bf16[2,384,256]{2,1,0:T(8,128)(2,1)} %bitcast.21, ...), custom_call_target="tpu_custom_call" | custom-call | tf_op jit(solution)/shard_map/ring_attention/pallas_call | solution.py:477
  218.5 0.0 copy-start.3
  218.5 0.0 copy-start
  218.5 3.9 %copy.11 = bf16[2,384,4,256]{3,2,1,0:T(4,128)(2,1)} copy(bf16[2,384,4,256]{3,1,2,0:T(8,128)(2,1)} %bitcast.18) | data formatting | bytes 3145728
  222.4 0.0 copy-done.3
  222.4 0.6 copy.19
  223.0 0.0 copy-done
  223.0 0.0 copy-start.2
  223.0 0.0 copy-start.1
  223.0 2.4 %copy.12 = bf16[2,384,4,256]{3,2,1,0:T(4,128)(2,1)} copy(bf16[2,384,4,256]{3,1,2,0:T(8,128)(2,1)S(1)} %bitcast.17) | data formatting | bytes 3145728
  225.4 0.0 copy-done.2
  225.4 0.7 copy.22
  226.1 0.0 copy-done.1
  226.1 0.7 copy.23
Async XLA Ops:
  218.5 3.9 %copy-start.3 = (f32[2,4,1,384]{3,2,1,0:T(1,128)S(1)}, f32[2,4,1,384]{3,2,1,0:T(1,128)}, u32[]{:S(2)}) copy-start(f32[2,4,1,384]{3,2,1,0:T(1,128)} %get-tuple-element.11) | copy-start | bytes 36868
  218.5 4.5 %copy-start = (bf16[2,4,384,256]{3,2,1,0:T(8,128)(2,1)S(1)}, bf16[2,4,384,256]{3,2,1,0:T(8,128)(2,1)}, u32[]{:S(2)}) copy-start(bf16[2,4,384,256]{3,2,1,0:T(8,128)(2,1)} %get-tuple-element.12) | copy-start | bytes 4718596
  223.0 2.4 %copy-start.2 = (bf16[2,384,256]{2,1,0:T(8,128)(2,1)S(1)}, bf16[2,384,256]{2,1,0:T(8,128)(2,1)}, u32[]{:S(2)}) copy-start(bf16[2,384,256]{2,1,0:T(8,128)(2,1)} %get-tuple-element.13) | copy-start | bytes 1179652
  223.0 3.1 %copy-start.1 = (bf16[2,384,256]{2,1,0:T(8,128)(2,1)S(1)}, bf16[2,384,256]{2,1,0:T(8,128)(2,1)}, u32[]{:S(2)}) copy-start(bf16[2,384,256]{2,1,0:T(8,128)(2,1)} %get-tuple-element.14) | copy-start | bytes 1179652

commit v4 on v2

--- a/solution.py
+++ b/solution.py
@@ -11,6 +11,7 @@
 LOG2E = 1.4426950408889634
 LN2 = 0.6931471805599453
 TILE = 256
+GO_AT = 3
 
 
 def attention_kernel(n, scale, q_hbm, k_hbm, v_hbm, g_hbm, out_hbm, lse_hbm, dq_hbm, dk_hbm, dv_hbm,
@@ -79,18 +80,6 @@
         def _():
             kv_dn(a, 0, chip).start()
 
-    def sent_all():
-        for a in range(2):
-            for step in range(hops_up[a]):
-                @pl.when(sends_up(a, step))
-                def _():
-                    kv_up(a, step, 0).wait_send()
-
-            for step in range(hops_dn[a]):
-                @pl.when(sends_dn(a, step))
-                def _():
-                    kv_dn(a, step, 0).wait_send()
-
     for a in range(2):
         arrived(a)
 
@@ -156,7 +145,7 @@
                     acc[h, :, cols] = acc[h, :, cols] * alpha + part
             return 0
 
-        lax.fori_loop(0, heads, head, 0)
+        lax.fori_loop(0, heads, head, 0, unroll=True)
 
     arrived(2)
 
@@ -202,11 +191,10 @@
         @pl.when(last)
         def _():
             take_dn(1, step)
-            sent_all()
-
-            @pl.when(core == 0)
-            def _():
-                pl.semaphore_signal(go_sem, inc=1, device_id={"cp": peer}, device_id_type=MESH)
+
+        @pl.when((core == 0) & (s == GO_AT))
+        def _():
+            pl.semaphore_signal(go_sem, inc=1, device_id={"cp": peer}, device_id_type=MESH)
 
         j = jnp.where(up, chip - 1 - step, (chip + 1 + step) % n)
         valid = (j >= 0) & (j < chip) & (up | (j < hops_dn[0]))
@@ -252,21 +240,31 @@
         dv_sum[j] = jnp.zeros((chunk, head_dim), jnp.float32)
 
         def head(h, _):
+            size = [(i + 1) * TILE if diagonal else chunk for i in range(tiles)]
+            cols = [slice(i * TILE, (i + 1) * TILE) for i in range(tiles)]
+            ps, dss = [], []
             for i in range(tiles):
-                cols = slice(i * TILE, (i + 1) * TILE)
-                rows = (i + 1) * TILE if diagonal else chunk
-                s = jnp.dot(k_all[j, :rows, :], q_t[h, :, cols], preferred_element_type=jnp.float32) * fold
+                s = jnp.dot(k_all[j, :size[i], :], q_t[h, :, cols[i]], preferred_element_type=jnp.float32)
+                dp = jnp.dot(v_all[j, :size[i], :], g_t[h, :, cols[i]], preferred_element_type=jnp.float32)
                 if diagonal:
-                    s = jnp.where(causal(rows, i), s, -jnp.inf)
-                p = jnp.exp2(s - run_m[h, :, cols])
-                dp = jnp.dot(v_all[j, :rows, :], g_t[h, :, cols], preferred_element_type=jnp.float32)
-                ds = (p * (dp - delta[h, :, cols])).astype(jnp.bfloat16)
-                dv_sum[j, :rows, :] += jnp.dot(p.astype(jnp.bfloat16), g_s[h, cols, :], preferred_element_type=jnp.float32)
-                dk_sum[j, :rows, :] += jnp.dot(ds, q_s[h, cols, :], preferred_element_type=jnp.float32)
-                acc[h, :, cols] += jnp.dot(turned[:, :rows], ds, preferred_element_type=jnp.float32)
+                    s = jnp.where(causal(size[i], i), s, -jnp.inf)
+                p = jnp.exp2(s * fold - run_m[h, :, cols[i]])
+                ps.append(p.astype(jnp.bfloat16))
+                dss.append((p * (dp - delta[h, :, cols[i]])).astype(jnp.bfloat16))
+            if diagonal:
+                for i in range(tiles):
+                    dv_sum[j, :size[i], :] += jnp.dot(ps[i], g_s[h, cols[i], :], preferred_element_type=jnp.float32)
+                    dk_sum[j, :size[i], :] += jnp.dot(dss[i], q_s[h, cols[i], :], preferred_element_type=jnp.float32)
+                    acc[h, :, cols[i]] += jnp.dot(turned[:, :size[i]], dss[i], preferred_element_type=jnp.float32)
+            else:
+                pp = jnp.concatenate(ps, axis=1)
+                dd = jnp.concatenate(dss, axis=1)
+                dv_sum[j] += jnp.dot(pp, g_s[h], preferred_element_type=jnp.float32)
+                dk_sum[j] += jnp.dot(dd, q_s[h], preferred_element_type=jnp.float32)
+                acc[h] += jnp.dot(turned[...], dd, preferred_element_type=jnp.float32)
             return 0
 
-        lax.fori_loop(0, heads, head, 0)
+        lax.fori_loop(0, heads, head, 0, unroll=2)
 
     def sum_dn(a, step, j):
         return remote(sums[a].at[j], from_up[a].at[step], dkv_dn_send.at[a, step], dkv_dn_recv.at[a, step], below)
@@ -275,13 +273,14 @@
         return remote(src, from_dn[a].at[step], dkv_up_send.at[a, step], dkv_up_recv.at[a, step], above)
 
     wide = n // 2
+    wrap = False
 
     def gives_dn(a, step):
-        skip = (a == 0) & (step == 0) & (chip == n - 1)
+        skip = (a == 0) & (step == 0) & (chip == n - 1) & wrap
         return (chip - hops_up[a] + step >= 0) & (step < hops_up[a]) & jnp.logical_not(skip)
 
     def gets_dn(a, step):
-        skip = (a == 0) & (step == 1) & (chip == n - 2)
+        skip = (a == 0) & (step == 1) & (chip == n - 2) & wrap
         return (step >= 1) & (chip < n - 1) & jnp.logical_not(skip)
 
     def up_index(step):
@@ -289,7 +288,10 @@
 
     def gives_up(a, step):
         j = up_index(step)
-        return (j < wide) & (j != chip) & (step < wide) & ((a == 1) | (step >= 1) | (chip == n - 1))
+        in_reach = (j < wide) & (j != chip) & (step < wide)
+        if a == 0:
+            in_reach &= (wrap & (chip == n - 1)) | ((step >= 1) & (wrap | (j < wide - 1)))
+        return in_reach
 
     def gets_up(a, step):
         return (step >= 2 - a) | ((step >= 1) & (up_index(step) > chip))
@@ -380,7 +382,7 @@
     pending.append(give_back(2, dq_s.at[:, mine], dq_s.at[:, theirs], dq_hbm))
 
     for a in range(2):
-        @pl.when(chip < wide)
+        @pl.when((chip < wide) if a == 1 else (chip < wide - 1) | (wrap & (chip < wide)))
         def _():
             sum_up(a, wide - 1, sums[a].at[chip]).wait_recv()
             add_in(a, chip, from_dn[a][wide - 1])
@@ -401,9 +403,18 @@
         swaps[i].wait_send()
     for a in range(2):
         for step in range(hops_up[a]):
+            @pl.when(sends_up(a, step))
+            def _():
+                kv_up(a, step, 0).wait_send()
+
             @pl.when(gives_dn(a, step))
             def _():
                 sum_dn(a, step, 0).wait_send()
+
+        for step in range(hops_dn[a]):
+            @pl.when(sends_dn(a, step))
+            def _():
+                kv_dn(a, step, 0).wait_send()
 
         for step in range(wide):
             @pl.when(gives_up(a, step))

time: 227 us -> 214 us (0.943)
  Pallas kernels: 214 us -> 201 us
    pallas_call x1, Pallas kernels: 214 us -> 201 us  [attention_shard(): pl.pallas_call(functools.partial(attention_kernel, chips, head_dim ** (-0...]
where the time goes in v4:
time: 214 us
  Pallas kernels  201 us (94%)
  local copies, waits for them, and re-layouts  12.4 us (6%)
    pallas_call x1, Pallas kernels, attention_shard(): pl.pallas_call(functools.partial(attention_kernel, chips, head_dim ** (-0...  201 us
    unnamed x13, local copies, waits for them, and re-layouts  8.35 us

profile of v4, /device:TPU:21, one launch (start us, length us, event | category | flops | bytes accessed | tf_op | source)
XLA Modules:
  0.0 214.0 jit_solution(1291786673329948075)
XLA Ops:
  0.6 4.1 %copy_bitcast_fusion = (bf16[2,4,384,256]{3,2,1,0:T(8,128)(2,1)}, bf16[2,4,384,256]{3,2,1,0:T(8,128)(2,1)}) fusion(bf16[2,384,4,256]{3,2,1,0:T(4,128)(2,1)} %param.7, bf16[2,384,4,256]{3,2,1,0:T(4,128)(2,1)} %param.4), kind=kLoop, calls=%fused_computation | loop fusion | bytes 6291456 | tf_op jit(solution)/shard_map/transpose | solution.py:438
  4.7 200.9 %ring_attention.1 = (bf16[2,4,384,256]{3,2,1,0:T(8,128)(2,1)}, f32[2,4,1,384]{3,2,1,0:T(1,128)}, bf16[2,4,384,256]{3,2,1,0:T(8,128)(2,1)}, bf16[2,384,256]{2,1,0:T(8,128)(2,1)}, bf16[2,384,256]{2,1,0:T(8,128)(2,1)}) custom-call(bf16[2,4,384,256]{3,2,1,0:T(8,128)(2,1)} %get-tuple-element.21.q_hbm, bf16[2,384,256]{2,1,0:T(8,128)(2,1)} %bitcast.21, ...), custom_call_target="tpu_custom_call" | custom-call | tf_op jit(solution)/shard_map/ring_attention/pallas_call | solution.py:443
  205.6 0.0 copy-start.3
  205.6 0.0 copy-start
  205.7 3.9 %copy.11 = bf16[2,384,4,256]{3,2,1,0:T(4,128)(2,1)} copy(bf16[2,384,4,256]{3,1,2,0:T(8,128)(2,1)} %bitcast.18) | data formatting | bytes 3145728
  209.5 0.0 copy-done.3
  209.5 0.6 copy.19
  210.1 0.0 copy-done
  210.1 0.0 copy-start.2
  210.1 0.0 copy-start.1
  210.1 2.4 %copy.12 = bf16[2,384,4,256]{3,2,1,0:T(4,128)(2,1)} copy(bf16[2,384,4,256]{3,1,2,0:T(8,128)(2,1)S(1)} %bitcast.17) | data formatting | bytes 3145728
  212.5 0.0 copy-done.2
  212.5 0.7 copy.22
  213.3 0.0 copy-done.1
  213.3 0.7 copy.23
Async XLA Ops:
  205.6 3.9 %copy-start.3 = (f32[2,4,1,384]{3,2,1,0:T(1,128)S(1)}, f32[2,4,1,384]{3,2,1,0:T(1,128)}, u32[]{:S(2)}) copy-start(f32[2,4,1,384]{3,2,1,0:T(1,128)} %get-tuple-element.11) | copy-start | bytes 36868
  205.6 4.5 %copy-start = (bf16[2,4,384,256]{3,2,1,0:T(8,128)(2,1)S(1)}, bf16[2,4,384,256]{3,2,1,0:T(8,128)(2,1)}, u32[]{:S(2)}) copy-start(bf16[2,4,384,256]{3,2,1,0:T(8,128)(2,1)} %get-tuple-element.12) | copy-start | bytes 4718596
  210.1 2.4 %copy-start.2 = (bf16[2,384,256]{2,1,0:T(8,128)(2,1)S(1)}, bf16[2,384,256]{2,1,0:T(8,128)(2,1)}, u32[]{:S(2)}) copy-start(bf16[2,384,256]{2,1,0:T(8,128)(2,1)} %get-tuple-element.13) | copy-start | bytes 1179652
  210.1 3.1 %copy-start.1 = (bf16[2,384,256]{2,1,0:T(8,128)(2,1)S(1)}, bf16[2,384,256]{2,1,0:T(8,128)(2,1)}, u32[]{:S(2)}) copy-start(bf16[2,384,256]{2,1,0:T(8,128)(2,1)} %get-tuple-element.14) | copy-start | bytes 1179652

commit v5 on v4

--- a/solution.py
+++ b/solution.py
@@ -11,7 +11,7 @@
 LOG2E = 1.4426950408889634
 LN2 = 0.6931471805599453
 TILE = 256
-GO_AT = 3
+GO_AT = 1
 
 
 def attention_kernel(n, scale, q_hbm, k_hbm, v_hbm, g_hbm, out_hbm, lse_hbm, dq_hbm, dk_hbm, dv_hbm,
@@ -173,39 +173,29 @@
         send_own(0)
         send_own(1)
 
-    def forward_pos(s, _):
-        step = s // 2
-        up = s % 2 == 0
-        last = s == n - 2
-
-        @pl.when(up)
-        def _():
-            take_up(0, step)
-            take_up(1, step)
-
-        @pl.when(jnp.logical_not(up))
-        def _():
-            take_dn(0, step)
-            take_dn(1, step)
-
-        @pl.when(last)
-        def _():
-            take_dn(1, step)
-
-        @pl.when((core == 0) & (s == GO_AT))
+    def forward_step(step, _):
+        for a in range(2):
+            take_up(a, step)
+            take_dn(a, step)
+
+        @pl.when((core == 0) & (step == GO_AT))
         def _():
             pl.semaphore_signal(go_sem, inc=1, device_id={"cp": peer}, device_id_type=MESH)
 
-        j = jnp.where(up, chip - 1 - step, (chip + 1 + step) % n)
-        valid = (j >= 0) & (j < chip) & (up | (j < hops_dn[0]))
-
-        @pl.when(valid)
-        def _():
-            forward_chunk(j, False)
-
-        return 0
-
-    lax.fori_loop(0, n - 1, forward_pos, 0)
+        def use(side, _):
+            j = jnp.where(side == 0, chip - 1 - step, (chip + 1 + step) % n)
+            valid = (j >= 0) & (j < chip) & ((side == 0) | ((j < hops_dn[0]) & (step < hops_dn[0])))
+
+            @pl.when(valid)
+            def _():
+                forward_chunk(j, False)
+
+            return 0
+
+        lax.fori_loop(0, 2, use, 0)
+        return 0
+
+    lax.fori_loop(0, n // 2, forward_step, 0)
 
     def finish(h, _):
         for i in range(tiles):

time: 214 us -> 208 us (0.972)
  Pallas kernels: 201 us -> 195 us
    pallas_call x1, Pallas kernels: 201 us -> 195 us  [attention_shard(): pl.pallas_call(functools.partial(attention_kernel, chips, head_dim ** (-0...]
where the time goes in v5:
time: 208 us
  Pallas kernels  195 us (94%)
  local copies, waits for them, and re-layouts  12.4 us (6%)
    pallas_call x1, Pallas kernels, attention_shard(): pl.pallas_call(functools.partial(attention_kernel, chips, head_dim ** (-0...  195 us
    unnamed x13, local copies, waits for them, and re-layouts  8.35 us

profile of v5, /device:TPU:21, one launch (start us, length us, event | category | flops | bytes accessed | tf_op | source)
XLA Modules:
  0.0 207.8 jit_solution(15556596590384793714)
XLA Ops:
  0.6 4.1 %copy_bitcast_fusion = (bf16[2,4,384,256]{3,2,1,0:T(8,128)(2,1)}, bf16[2,4,384,256]{3,2,1,0:T(8,128)(2,1)}) fusion(bf16[2,384,4,256]{3,2,1,0:T(4,128)(2,1)} %param.7, bf16[2,384,4,256]{3,2,1,0:T(4,128)(2,1)} %param.4), kind=kLoop, calls=%fused_computation | loop fusion | bytes 6291456 | tf_op jit(solution)/shard_map/transpose | solution.py:428
  4.7 194.7 %ring_attention.1 = (bf16[2,4,384,256]{3,2,1,0:T(8,128)(2,1)}, f32[2,4,1,384]{3,2,1,0:T(1,128)}, bf16[2,4,384,256]{3,2,1,0:T(8,128)(2,1)}, bf16[2,384,256]{2,1,0:T(8,128)(2,1)}, bf16[2,384,256]{2,1,0:T(8,128)(2,1)}) custom-call(bf16[2,4,384,256]{3,2,1,0:T(8,128)(2,1)} %get-tuple-element.21.q_hbm, bf16[2,384,256]{2,1,0:T(8,128)(2,1)} %bitcast.21, ...), custom_call_target="tpu_custom_call" | custom-call | tf_op jit(solution)/shard_map/ring_attention/pallas_call | solution.py:433
  199.4 0.0 copy-start.3
  199.4 0.0 copy-start
  199.4 3.9 %copy.11 = bf16[2,384,4,256]{3,2,1,0:T(4,128)(2,1)} copy(bf16[2,384,4,256]{3,1,2,0:T(8,128)(2,1)} %bitcast.18) | data formatting | bytes 3145728
  203.3 0.0 copy-done.3
  203.3 0.6 copy.19
  203.9 0.0 copy-done
  203.9 0.0 copy-start.2
  203.9 0.0 copy-start.1
  203.9 2.4 %copy.12 = bf16[2,384,4,256]{3,2,1,0:T(4,128)(2,1)} copy(bf16[2,384,4,256]{3,1,2,0:T(8,128)(2,1)S(1)} %bitcast.17) | data formatting | bytes 3145728
  206.3 0.0 copy-done.2
  206.3 0.7 copy.22
  207.0 0.0 copy-done.1
  207.0 0.7 copy.23
Async XLA Ops:
  199.4 3.9 %copy-start.3 = (f32[2,4,1,384]{3,2,1,0:T(1,128)S(1)}, f32[2,4,1,384]{3,2,1,0:T(1,128)}, u32[]{:S(2)}) copy-start(f32[2,4,1,384]{3,2,1,0:T(1,128)} %get-tuple-element.11) | copy-start | bytes 36868
  199.4 4.5 %copy-start = (bf16[2,4,384,256]{3,2,1,0:T(8,128)(2,1)S(1)}, bf16[2,4,384,256]{3,2,1,0:T(8,128)(2,1)}, u32[]{:S(2)}) copy-start(bf16[2,4,384,256]{3,2,1,0:T(8,128)(2,1)} %get-tuple-element.12) | copy-start | bytes 4718596
  203.9 2.4 %copy-start.2 = (bf16[2,384,256]{2,1,0:T(8,128)(2,1)S(1)}, bf16[2,384,256]{2,1,0:T(8,128)(2,1)}, u32[]{:S(2)}) copy-start(bf16[2,384,256]{2,1,0:T(8,128)(2,1)} %get-tuple-element.13) | copy-start | bytes 1179652
  203.9 3.1 %copy-start.1 = (bf16[2,384,256]{2,1,0:T(8,128)(2,1)S(1)}, bf16[2,384,256]{2,1,0:T(8,128)(2,1)}, u32[]{:S(2)}) copy-start(bf16[2,384,256]{2,1,0:T(8,128)(2,1)} %get-tuple-element.14) | copy-start | bytes 1179652

commit v6 on v5

--- a/solution.py
+++ b/solution.py
@@ -15,7 +15,7 @@
 
 
 def attention_kernel(n, scale, q_hbm, k_hbm, v_hbm, g_hbm, out_hbm, lse_hbm, dq_hbm, dk_hbm, dv_hbm,
-                     k_all, v_all, turned, q_s, q_t, g_s, g_t, acc, run_m, run_l, delta, lse_s, out_s, dq_s, dk_s, dv_s,
+                     k_all, v_all, turned, q_s, q_t, g_s, g_t, acc, run_m, run_l, delta, lse_s, by_head, q_raw, g_raw, dk_s, dv_s,
                      dk_sum, dv_sum, dk_dn, dv_dn, dk_up, dv_up,
                      load_sem, swap_send, swap_recv, kv_up_send, kv_up_recv, kv_dn_send, kv_dn_recv,
                      dkv_dn_send, dkv_dn_recv, dkv_up_send, dkv_up_recv, store_sem, back_send, back_recv, go_sem):
@@ -47,7 +47,7 @@
         pl.semaphore_signal(barrier, inc=1, device_id={"cp": device}, device_id_type=MESH)
     pl.semaphore_wait(barrier, 3)
 
-    places = (k_all.at[chip, mine], v_all.at[chip, mine], q_s.at[:, mine], g_s.at[:, mine])
+    places = (k_all.at[chip, mine], v_all.at[chip, mine], q_raw.at[core], g_raw.at[core])
     sources = (k_hbm, v_hbm, q_hbm, g_hbm)
     swaps = [remote(sources[i].at[other], places[i], swap_send.at[i], swap_recv.at[i], peer) for i in range(4)]
     loads = [pltpu.make_async_copy(sources[i].at[core], places[i], load_sem.at[i]) for i in range(4)]
@@ -147,7 +147,16 @@
 
         lax.fori_loop(0, heads, head, 0, unroll=True)
 
+    def split_heads(src, dst):
+        for i in range(2):
+            dst[:, i * half:(i + 1) * half, :] = jnp.swapaxes(src[i], 0, 1)
+
+    def join_heads(src, dst):
+        for i in range(2):
+            dst[i] = jnp.swapaxes(src[:, i * half:(i + 1) * half, :], 0, 1)
+
     arrived(2)
+    split_heads(q_raw, q_s)
 
     def turn_q(h, _):
         for i in range(tiles):
@@ -158,6 +167,7 @@
     lax.fori_loop(0, heads, turn_q, 0)
     forward_chunk(chip, True)
     arrived(3)
+    split_heads(g_raw, g_s)
 
     def turn_g(h, _):
         for i in range(tiles):
@@ -207,10 +217,11 @@
             lse2 = run_m[h, :, cols] + jnp.log2(total)
             run_m[h, :, cols] = lse2
             lse_s[h, :, cols] = lse2 * LN2
-            out_s[h, cols, :] = out.T
+            by_head[h, cols, :] = out.T
         return 0
 
     lax.fori_loop(0, heads, finish, 0)
+    join_heads(by_head, q_raw)
 
     def give_back(i, src_mine, src_theirs, dst):
         swap = remote(src_theirs, dst.at[core], back_send.at[i], back_recv.at[i], peer)
@@ -220,7 +231,7 @@
         return swap, keep
 
     pending = [
-        give_back(0, out_s.at[:, mine], out_s.at[:, theirs], out_hbm),
+        give_back(0, q_raw.at[core], q_raw.at[other], out_hbm),
         give_back(1, lse_s.at[:, :, mine], lse_s.at[:, :, theirs], lse_hbm),
     ]
 
@@ -365,11 +376,12 @@
     def finish_q(h, _):
         for i in range(tiles):
             cols = slice(i * TILE, (i + 1) * TILE)
-            dq_s[h, cols, :] = (acc[h, :, cols] * scale).astype(jnp.bfloat16).T
+            by_head[h, cols, :] = (acc[h, :, cols] * scale).astype(jnp.bfloat16).T
         return 0
 
     lax.fori_loop(0, heads, finish_q, 0)
-    pending.append(give_back(2, dq_s.at[:, mine], dq_s.at[:, theirs], dq_hbm))
+    join_heads(by_head, g_raw)
+    pending.append(give_back(2, g_raw.at[core], g_raw.at[other], dq_hbm))
 
     for a in range(2):
         @pl.when((chip < wide) if a == 1 else (chip < wide - 1) | (wrap & (chip < wide)))
@@ -424,8 +436,6 @@
         chunk = 2 * tokens
         half = chips // 2
         bf16, f32 = jnp.bfloat16, jnp.float32
-        q = jnp.transpose(queries, (0, 2, 1, 3))
-        g = jnp.transpose(out_grad, (0, 2, 1, 3))
         k = keys.reshape(batch, tokens, head_dim)
         v = values.reshape(batch, tokens, head_dim)
         any_spec = pl.BlockSpec(memory_space=pl.ANY)
@@ -433,9 +443,9 @@
         out, lse, dq, dk, dv = pl.pallas_call(
             functools.partial(attention_kernel, chips, head_dim ** -0.5),
             out_shape=(
-                jax.ShapeDtypeStruct(q.shape, bf16),
+                jax.ShapeDtypeStruct(queries.shape, bf16),
                 jax.ShapeDtypeStruct((batch, heads, 1, tokens), f32),
-                jax.ShapeDtypeStruct(q.shape, bf16),
+                jax.ShapeDtypeStruct(queries.shape, bf16),
                 jax.ShapeDtypeStruct(k.shape, bf16),
                 jax.ShapeDtypeStruct(k.shape, bf16),
             ),
@@ -455,7 +465,8 @@
                 pltpu.VMEM((heads, 1, chunk), f32),
                 pltpu.VMEM((heads, 1, chunk), f32),
                 pltpu.VMEM((heads, chunk, head_dim), bf16),
-                pltpu.VMEM((heads, chunk, head_dim), bf16),
+                pltpu.VMEM((2, tokens, heads, head_dim), bf16),
+                pltpu.VMEM((2, tokens, heads, head_dim), bf16),
                 pltpu.VMEM((chunk, head_dim), bf16),
                 pltpu.VMEM((chunk, head_dim), bf16),
                 pltpu.VMEM((chips, chunk, head_dim), f32),
@@ -471,12 +482,11 @@
             ],
             compiler_params=pltpu.CompilerParams(collective_id=0, has_side_effects=True, vmem_limit_bytes=67043328),
             name="ring_attention",
-        )(q, k, v, g)
-        back = (0, 2, 1, 3)
+        )(queries, k, v, out_grad)
         return (
-            jnp.transpose(out, back),
+            out,
             lse.reshape(batch, heads, tokens),
-            jnp.transpose(dq, back),
+            dq,
             dk.reshape(keys.shape),
             dv.reshape(values.shape),
         )

time: 208 us -> 203 us (0.976)
  local copies, waits for them, and re-layouts: 12.4 us -> 7.25 us
    transpose x1 -> x0, local copies, waits for them, and re-layouts: 4.09 us -> none  [attention_shard(): g = jnp.transpose(out_grad, (0, 2, 1, 3))]
    unnamed x13 -> x11, local copies, waits for them, and re-layouts: 8.35 us -> 7.25 us
where the time goes in v6:
time: 203 us
  Pallas kernels  195 us (96%)
  local copies, waits for them, and re-layouts  7.25 us (4%)
    pallas_call x1, Pallas kernels, attention_shard(): pl.pallas_call(functools.partial(attention_kernel, chips, head_dim ** (-0...  195 us
    unnamed x11, local copies, waits for them, and re-layouts  7.25 us

profile of v6, /device:TPU:21, one launch (start us, length us, event | category | flops | bytes accessed | tf_op | source)
XLA Modules:
  0.0 203.0 jit_solution(5989003499135825243)
XLA Ops:
  0.6 195.1 %ring_attention.1 = (bf16[2,384,4,256]{3,2,1,0:T(4,128)(2,1)}, f32[2,4,1,384]{3,2,1,0:T(1,128)}, bf16[2,384,4,256]{3,2,1,0:T(4,128)(2,1)}, bf16[2,384,256]{2,1,0:T(8,128)(2,1)}, bf16[2,384,256]{2,1,0:T(8,128)(2,1)}) custom-call(bf16[2,384,4,256]{3,2,1,0:T(4,128)(2,1)} %q_hbm.1, bf16[2,384,256]{2,1,0:T(8,128)(2,1)} %bitcast.13, ...), custom_call_target="tpu_custom_call" | custom-call | tf_op jit(solution)/shard_map/ring_attention/pallas_call | solution.py:443
  195.8 1.3 copy.13
  197.1 0.0 copy-start
  197.1 3.2 %copy.18 = bf16[2,384,4,256]{3,2,1,0:T(4,128)(2,1)} copy(bf16[2,384,4,256]{3,2,1,0:T(4,128)(2,1)} %get-tuple-element.25) | data formatting | bytes 3145728
  200.3 0.0 copy-done
  200.3 0.0 copy-start.2
  200.3 0.0 copy-start.1
  200.3 1.1 copy.19
  201.5 0.1 copy-done.2
  201.5 0.7 copy.20
  202.3 0.0 copy-done.1
  202.3 0.7 copy.21
Async XLA Ops:
  197.1 3.2 %copy-start = (bf16[2,384,4,256]{3,2,1,0:T(4,128)(2,1)S(1)}, bf16[2,384,4,256]{3,2,1,0:T(4,128)(2,1)}, u32[]{:S(2)}) copy-start(bf16[2,384,4,256]{3,2,1,0:T(4,128)(2,1)} %get-tuple-element.27) | copy-start | bytes 4718596
  200.3 1.2 copy-start.2
  200.3 2.0 copy-start.1

commit v7 on v6

--- a/solution.py
+++ b/solution.py
@@ -11,7 +11,7 @@
 LOG2E = 1.4426950408889634
 LN2 = 0.6931471805599453
 TILE = 256
-GO_AT = 1
+GO_AT = 2
 
 
 def attention_kernel(n, scale, q_hbm, k_hbm, v_hbm, g_hbm, out_hbm, lse_hbm, dq_hbm, dk_hbm, dv_hbm,
@@ -426,6 +426,22 @@
     for swap, keep in pending:
         keep.wait()
         swap.wait()
+
+
+def place_kernel(lse_in, out_in, dq_in, dk_in, dv_in, lse_out, out_out, dq_out, dk_out, dv_out, out_buf, dq_buf, dk_buf, dv_buf, in_sem, out_sem):
+    pieces = []
+    for src, buf, dst in ((out_in, out_buf, out_out), (dq_in, dq_buf, dq_out), (dk_in, dk_buf, dk_out), (dv_in, dv_buf, dv_out)):
+        for b in range(src.shape[0]):
+            i = len(pieces)
+            pieces.append((pltpu.make_async_copy(src.at[b], buf.at[b], in_sem.at[i]), pltpu.make_async_copy(buf.at[b], dst.at[b], out_sem.at[i])))
+    for load, _ in pieces:
+        load.start()
+    lse_out[...] = lse_in[:, :, 0, :]
+    for load, store in pieces:
+        load.wait()
+        store.start()
+    for _, store in pieces:
+        store.wait()
 
 
 def solution(mesh):
@@ -483,13 +499,17 @@
             compiler_params=pltpu.CompilerParams(collective_id=0, has_side_effects=True, vmem_limit_bytes=67043328),
             name="ring_attention",
         )(queries, k, v, out_grad)
-        return (
-            out,
-            lse.reshape(batch, heads, tokens),
-            dq,
-            dk.reshape(keys.shape),
-            dv.reshape(values.shape),
-        )
+        vmem_spec = pl.BlockSpec(memory_space=pltpu.VMEM)
+        results = (out, dq, dk, dv)
+        row_lse, out, dq, dk, dv = pl.pallas_call(
+            place_kernel,
+            out_shape=(jax.ShapeDtypeStruct((batch, heads, tokens), f32),) + tuple(jax.ShapeDtypeStruct(x.shape, bf16) for x in results),
+            in_specs=[vmem_spec] + [any_spec] * 4,
+            out_specs=(vmem_spec,) + (any_spec,) * 4,
+            scratch_shapes=[pltpu.VMEM(x.shape, bf16) for x in results] + [dma((4 * batch,)), dma((4 * batch,))],
+            name="place_results",
+        )(lse, *results)
+        return out, row_lse, dq, dk.reshape(keys.shape), dv.reshape(values.shape)
 
     seq_spec = P("dp", "cp")
     return jax.shard_map(attention_shard, mesh=mesh, in_specs=(seq_spec,) * 4, out_specs=(seq_spec, P("dp", None, "cp"), seq_spec, seq_spec, seq_spec), check_vma=False)

time: 203 us -> 197 us (0.970)
  local copies, waits for them, and re-layouts: 7.25 us -> 0 us
    unnamed x11 -> x0, local copies, waits for them, and re-layouts: 7.25 us -> none
    pallas_call x0 -> x1, Pallas kernels: none -> 4.48 us  [attention_shard(): pl.pallas_call(place_kernel, out_shape=(jax.ShapeDtypeStruct((batch, head...]
    pallas_call x1, Pallas kernels: 195 us -> 191 us  [attention_shard(): pl.pallas_call(functools.partial(attention_kernel, chips, head_dim ** (-0...]
where the time goes in v7:
time: 197 us
  Pallas kernels  196 us (99%)
    pallas_call x1, Pallas kernels, attention_shard(): pl.pallas_call(functools.partial(attention_kernel, chips, head_dim ** (-0...  191 us
    pallas_call x1, Pallas kernels, attention_shard(): pl.pallas_call(place_kernel, out_shape=(jax.ShapeDtypeStruct((batch, head...  4.48 us

profile of v7, /device:TPU:21, one launch (start us, length us, event | category | flops | bytes accessed | tf_op | source)
XLA Modules:
  0.0 196.7 jit_solution(4081200270480442946)
XLA Ops:
  0.6 191.5 %ring_attention.1 = (bf16[2,384,4,256]{3,2,1,0:T(4,128)(2,1)}, f32[2,4,1,384]{3,2,1,0:T(1,128)}, bf16[2,384,4,256]{3,2,1,0:T(4,128)(2,1)}, bf16[2,384,256]{2,1,0:T(8,128)(2,1)}, bf16[2,384,256]{2,1,0:T(8,128)(2,1)}) custom-call(bf16[2,384,4,256]{3,2,1,0:T(4,128)(2,1)} %q_hbm.1, bf16[2,384,256]{2,1,0:T(8,128)(2,1)} %bitcast.8, bf16[2,384,256]{2,1,0:T(8,128)(2,1)} %bitcast.9, ...), custom_call_target="tpu_custom_call" | custom-call | tf_op jit(solution)/shard_map/ring_attention/pallas_call | solution.py:459
  192.1 4.5 %place_results.1 = (f32[2,4,384]{2,1,0:T(4,128)}, bf16[2,384,4,256]{3,2,1,0:T(4,128)(2,1)}, bf16[2,384,4,256]{3,2,1,0:T(4,128)(2,1)}, bf16[2,384,256]{2,1,0:T(8,128)(2,1)}, bf16[2,384,256]{2,1,0:T(8,128)(2,1)}) custom-call(f32[2,4,1,384]{3,2,1,0:T(1,128)} %get-tuple-element.15.lse_in, bf16[2,384,4,256]{3,2,1,0:T(4,128)(2,1)} %get-tuple-element.16.out_in, ...), custom_call_target="tpu_custom_call" | custom-call | tf_op jit(solution)/shard_map/place_results/pallas_call | solution.py:504

commit v8 on v7

--- a/solution.py
+++ b/solution.py
@@ -265,7 +265,7 @@
                 acc[h] += jnp.dot(turned[...], dd, preferred_element_type=jnp.float32)
             return 0
 
-        lax.fori_loop(0, heads, head, 0, unroll=2)
+        lax.fori_loop(0, heads, head, 0, unroll=True)
 
     def sum_dn(a, step, j):
         return remote(sums[a].at[j], from_up[a].at[step], dkv_dn_send.at[a, step], dkv_dn_recv.at[a, step], below)
@@ -428,20 +428,27 @@
         swap.wait()
 
 
-def place_kernel(lse_in, out_in, dq_in, dk_in, dv_in, lse_out, out_out, dq_out, dk_out, dv_out, out_buf, dq_buf, dk_buf, dv_buf, in_sem, out_sem):
+def place_kernel(lse_in, out_in, dq_in, dk_in, dv_in, lse_out, out_out, dq_out, dk_out, dv_out, lse_buf, row_buf, out_buf, dq_buf, dk_buf, dv_buf, in_sem, out_sem):
     pieces = []
     for src, buf, dst in ((out_in, out_buf, out_out), (dq_in, dq_buf, dq_out), (dk_in, dk_buf, dk_out), (dv_in, dv_buf, dv_out)):
         for b in range(src.shape[0]):
             i = len(pieces)
             pieces.append((pltpu.make_async_copy(src.at[b], buf.at[b], in_sem.at[i]), pltpu.make_async_copy(buf.at[b], dst.at[b], out_sem.at[i])))
+    last = len(pieces)
+    lse_load = pltpu.make_async_copy(lse_in, lse_buf, in_sem.at[last])
+    lse_store = pltpu.make_async_copy(row_buf, lse_out, out_sem.at[last])
+    lse_load.start()
     for load, _ in pieces:
         load.start()
-    lse_out[...] = lse_in[:, :, 0, :]
+    lse_load.wait()
+    row_buf[...] = lse_buf[:, :, 0, :]
     for load, store in pieces:
         load.wait()
         store.start()
+    lse_store.start()
     for _, store in pieces:
         store.wait()
+    lse_store.wait()
 
 
 def solution(mesh):
@@ -499,14 +506,13 @@
             compiler_params=pltpu.CompilerParams(collective_id=0, has_side_effects=True, vmem_limit_bytes=67043328),
             name="ring_attention",
         )(queries, k, v, out_grad)
-        vmem_spec = pl.BlockSpec(memory_space=pltpu.VMEM)
         results = (out, dq, dk, dv)
         row_lse, out, dq, dk, dv = pl.pallas_call(
             place_kernel,
             out_shape=(jax.ShapeDtypeStruct((batch, heads, tokens), f32),) + tuple(jax.ShapeDtypeStruct(x.shape, bf16) for x in results),
-            in_specs=[vmem_spec] + [any_spec] * 4,
-            out_specs=(vmem_spec,) + (any_spec,) * 4,
-            scratch_shapes=[pltpu.VMEM(x.shape, bf16) for x in results] + [dma((4 * batch,)), dma((4 * batch,))],
+            in_specs=[any_spec] * 5,
+            out_specs=(any_spec,) * 5,
+            scratch_shapes=[pltpu.VMEM(lse.shape, f32), pltpu.VMEM((batch, heads, tokens), f32)] + [pltpu.VMEM(x.shape, bf16) for x in results] + [dma((4 * batch + 1,))] * 2,
             name="place_results",
         )(lse, *results)
         return out, row_lse, dq, dk.reshape(keys.shape), dv.reshape(values.shape)

time: 197 us -> 196 us (level)
  no operation moved by 1% of the time
where the time goes in v8:
time: 196 us; the launch traced here: 195 us
  Pallas kernels  195 us (99%)
    pallas_call x1, Pallas kernels, attention_shard(): pl.pallas_call(functools.partial(attention_kernel, chips, head_dim ** (-0...  191 us

profile of v8, /device:TPU:21, one launch (start us, length us, event | category | flops | bytes accessed | tf_op | source)
XLA Modules:
  0.0 195.5 jit_solution(8596444271614111259)
XLA Ops:
  0.6 191.5 %ring_attention.1 = (bf16[2,384,4,256]{3,2,1,0:T(4,128)(2,1)}, f32[2,4,1,384]{3,2,1,0:T(1,128)}, bf16[2,384,4,256]{3,2,1,0:T(4,128)(2,1)}, bf16[2,384,256]{2,1,0:T(8,128)(2,1)}, bf16[2,384,256]{2,1,0:T(8,128)(2,1)}) custom-call(bf16[2,384,4,256]{3,2,1,0:T(4,128)(2,1)} %q_hbm.1, bf16[2,384,256]{2,1,0:T(8,128)(2,1)} %bitcast.8, bf16[2,384,256]{2,1,0:T(8,128)(2,1)} %bitcast.9, ...), custom_call_target="tpu_custom_call" | custom-call | tf_op jit(solution)/shard_map/ring_attention/pallas_call | solution.py:466
  192.1 3.2 %place_results.1 = (f32[2,4,384]{2,1,0:T(4,128)}, bf16[2,384,4,256]{3,2,1,0:T(4,128)(2,1)}, bf16[2,384,4,256]{3,2,1,0:T(4,128)(2,1)}, bf16[2,384,256]{2,1,0:T(8,128)(2,1)}, bf16[2,384,256]{2,1,0:T(8,128)(2,1)}) custom-call(f32[2,4,1,384]{3,2,1,0:T(1,128)} %get-tuple-element.15.lse_in, bf16[2,384,4,256]{3,2,1,0:T(4,128)(2,1)} %get-tuple-element.16.out_in, ...), custom_call_target="tpu_custom_call" | custom-call | tf_op jit(solution)/shard_map/place_results/pallas_call | solution.py:510
